TPU v7x, 32 devices: a whole 2x2x4 slice. The times are simulated.
32 devices in a mesh: tm: 2 (over core), stn: 4 (over z), chan: 4 (over y, x).
Axes of the slice: x: 2, y: 2, z: 4, core: 2. Of those that a mesh axis runs over, the one named last changes fastest.
Arguments:
- voltages: bfloat16 [2, 8, 512, 32, 2, 256], P(None, 'chan', 'stn', 'tm'), may hold values from -100 to 100
- fir_taps: float32 [16, 256], replicated, may hold values from -1.5 to 1.5
- station_map: int32 [512], P('stn'), may hold values from 0 to 31, as said below
- beam_index: int32 [512], P('stn'), may hold values from 0 to 15
- weight_table: bfloat16 [2, 16, 8, 8], P(None, None, 'chan'), may hold values from -1.5 to 1.5
Outputs:
- visibilities: float32 [2, 2, 8, 32, 32, 8, 2, 2, 256], P('tm', None, 'chan', 'stn')
Inputs may be any that keep to these rules, and one draw needn't show every extreme that they name: `station_map`: each station number names exactly 16 dishes; of the dishes g * 128 up to (g + 1) * 128 - 1, exactly 32 name a station of the block h * 8 up to (h + 1) * 8 - 1, for every g and h.
All inputs are finite; a program needn't handle non-finite values.
Results may differ from a plain program's by a relative error of at most 0.017.
Values may be sent and summed in bfloat16 or wider, within the bound.
A program may use at most 512 MiB of HBM per device.

v0:
```python
import functools

import jax
import jax.numpy as jnp
from jax import lax
from jax.experimental import pallas as pl
from jax.experimental.pallas import tpu as pltpu
from jax.sharding import PartitionSpec as P

STATIONS = 32
COARSE = 8
LANES = 128
VMEM_LIMIT = 60 * 1024 * 1024

epsilon = 1e-06


def shifted(value, axis, steps):
    count = lax.axis_size(axis)
    first, last = (max(0, -steps), min(count, count - steps))
    return lax.ppermute(value, axis, [(source, source + steps) for source in range(first, last)])


def dft_table(length):
    bin_index = jnp.arange(length, dtype=jnp.int32)
    phase_step = bin_index[:, None] * bin_index[None, :] % length
    angles = phase_step.astype(jnp.float32) * (2.0 * jnp.pi / length)
    cosine = jnp.cos(angles).astype(jnp.bfloat16)
    sine = jnp.sin(angles).astype(jnp.bfloat16)
    top = jnp.concatenate([cosine, -sine], axis=1)
    return jnp.concatenate([top, jnp.concatenate([sine, cosine], axis=1)], axis=0)


def spectra_kernel(n_dest, x_ref, taps_ref, dft_ref, perm_ref, out_ref, fil_ref):
    taps = taps_ref.shape[0]
    frames = out_ref.shape[2]
    dishes, fine = x_ref.shape[3], x_ref.shape[4]
    share = dishes // n_dest
    rows = min(32, dishes)
    group = 2

    def step(i, carry):
        for j in range(group):
            frame = i * group + j
            for o in range(2):
                for low in range(0, dishes, rows):
                    total = jnp.zeros((rows, fine), jnp.float32)
                    for tap in range(taps):
                        sample = x_ref[0, frame + (taps - 1 - tap), o, low : low + rows, :]
                        total = total + taps_ref[tap : tap + 1, :] * sample.astype(jnp.float32)
                    fil_ref[
                        j * dishes + low : j * dishes + low + rows, o * fine : (o + 1) * fine
                    ] = total.astype(jnp.bfloat16)
        spec = jnp.dot(fil_ref[...], dft_ref[...], preferred_element_type=jnp.float32)
        spec = spec.astype(jnp.bfloat16)
        for j in range(group):
            moved = jnp.dot(
                perm_ref[...],
                spec[j * dishes : (j + 1) * dishes],
                preferred_element_type=jnp.float32,
            )
            for dest in range(n_dest):
                for o in range(2):
                    out_ref[dest, 0, i * group + j, o] = moved[
                        dest * share : (dest + 1) * share, o * fine : (o + 1) * fine
                    ].astype(jnp.bfloat16)
        return carry

    lax.fori_loop(0, frames // group, step, 0)


def spectra_of(extended, fir_taps, table, perm, n_dest, frames):
    polars, total_frames, _, dishes, fine = extended.shape
    share = dishes // n_dest
    flops = 2 * polars * frames * dishes * (2 * fine) * (2 * fine + dishes)
    return pl.pallas_call(
        functools.partial(spectra_kernel, n_dest),
        grid=(polars,),
        in_specs=[
            pl.BlockSpec((1, total_frames, 2, dishes, fine), lambda p: (p, 0, 0, 0, 0)),
            pl.BlockSpec(fir_taps.shape, lambda p: (0, 0)),
            pl.BlockSpec(table.shape, lambda p: (0, 0)),
            pl.BlockSpec(perm.shape, lambda p: (0, 0)),
        ],
        out_specs=pl.BlockSpec(
            (n_dest, 1, frames, 2, share, fine), lambda p: (0, p, 0, 0, 0, 0)
        ),
        out_shape=jax.ShapeDtypeStruct((n_dest, polars, frames, 2, share, fine), jnp.bfloat16),
        scratch_shapes=[pltpu.VMEM((2 * dishes, 2 * fine), jnp.bfloat16)],
        compiler_params=pltpu.CompilerParams(vmem_limit_bytes=VMEM_LIMIT),
        cost_estimate=pl.CostEstimate(
            flops=flops * 4, bytes_accessed=extended.size * 4, transcendentals=0
        ),
        name="spectra",
    )(extended, fir_taps, table, perm)


def beams_kernel(x_ref, steer_ref, out_ref, power_ref):
    frames, fine = out_ref.shape[1], out_ref.shape[3]
    power_ref[...] = jnp.zeros_like(power_ref)

    def step(frame, carry):
        terms = x_ref[:, 0, frame]
        if terms.shape[2] % 16:
            terms = terms.astype(jnp.float32).reshape(-1, fine).astype(jnp.bfloat16)
        else:
            terms = terms.reshape(-1, fine)
        formed = jnp.dot(steer_ref[...], terms, preferred_element_type=jnp.float32)
        formed = formed.astype(jnp.bfloat16)
        out_ref[0, frame] = formed
        wide = formed.astype(jnp.float32)
        power_ref[0] += wide * wide
        return carry

    lax.fori_loop(0, frames, step, 0)


def beams_of(spectra, steering):
    groups, polars, frames, _, share, fine = spectra.shape
    rows = steering.shape[0]
    return pl.pallas_call(
        beams_kernel,
        grid=(polars,),
        in_specs=[
            pl.BlockSpec((groups, 1, frames, 2, share, fine), lambda p: (0, p, 0, 0, 0, 0)),
            pl.BlockSpec(steering.shape, lambda p: (0, 0)),
        ],
        out_specs=[
            pl.BlockSpec((1, frames, rows, fine), lambda p: (p, 0, 0, 0)),
            pl.BlockSpec((1, rows, fine), lambda p: (p, 0, 0)),
        ],
        out_shape=[
            jax.ShapeDtypeStruct((polars, frames, rows, fine), jnp.bfloat16),
            jax.ShapeDtypeStruct((polars, rows, fine), jnp.float32),
        ],
        compiler_params=pltpu.CompilerParams(vmem_limit_bytes=VMEM_LIMIT),
        cost_estimate=pl.CostEstimate(
            flops=2 * rows * steering.shape[1] * polars * frames * fine,
            bytes_accessed=spectra.size * 4,
            transcendentals=0,
        ),
        name="beams",
    )(spectra, steering)


def correlate_kernel(beams, left_ref, right_ref, lscale_ref, rscale_ref, *rest):
    out_ref, left, right = rest[-3:]
    polars, frames, rows, fine = left_ref.shape
    own = rows // (2 * beams)
    halves = fine // LANES
    first = pl.program_id(0) == 0

    def widen(source, target):
        def step(i, carry):
            for p in range(polars):
                target[p, i] = source(p, i).astype(jnp.float32)
            return carry

        lax.fori_loop(0, frames, step, 0)

    @pl.when(first)
    def _():
        widen(lambda p, i: left_ref[p, i], left)

    widen(lambda p, i: right_ref[0, p, i], right)

    def pair(index, carry):
        s = index // own
        t = index % own
        srow = pl.multiple_of(s * (2 * beams), 2 * beams)
        trow = pl.multiple_of(t * (2 * beams), 2 * beams)
        for half in range(halves):
            lanes = pl.ds(half * LANES, LANES)
            re = {}
            im = {}
            for f in range(frames):
                lre = [left[p, f, pl.ds(srow, beams), lanes] for p in range(polars)]
                lim = [left[p, f, pl.ds(srow + beams, beams), lanes] for p in range(polars)]
                rre = [right[q, f, pl.ds(trow, beams), lanes] for q in range(polars)]
                rim = [right[q, f, pl.ds(trow + beams, beams), lanes] for q in range(polars)]
                for p in range(polars):
                    for q in range(polars):
                        a = lre[p] * rre[q] + lim[p] * rim[q]
                        b = lim[p] * rre[q] - lre[p] * rim[q]
                        re[p, q] = a if f == 0 else re[p, q] + a
                        im[p, q] = b if f == 0 else im[p, q] + b
            for p in range(polars):
                for q in range(polars):
                    scale = lscale_ref[p, s] * rscale_ref[0, q, t]
                    row = (p * halves + half) * polars + q
                    where = pl.ds(row, beams, stride=polars * polars * halves)
                    out_ref[0, 0, s, t, where, :] = re[p, q] * scale
                    out_ref[1, 0, s, t, where, :] = im[p, q] * scale
        return carry

    lax.fori_loop(0, own * own, pair, 0)


def correlate(index, coarse_dev, beams, left, right, lscale, rscale, previous):
    groups, polars, frames, rows, fine = right.shape
    own = rows // (2 * beams)
    out_rows = beams * polars * polars * (fine // LANES)
    shape = (2, coarse_dev, own, groups * own, out_rows, LANES)
    in_specs = [
        pl.BlockSpec((polars, frames, rows, fine), lambda g: (0, 0, 0, 0)),
        pl.BlockSpec((1, polars, frames, rows, fine), lambda g: (g, 0, 0, 0, 0)),
        pl.BlockSpec(lscale.shape, lambda g: (0, 0, 0, 0)),
        pl.BlockSpec((1,) + rscale.shape[1:], lambda g: (g, 0, 0, 0, 0)),
    ]
    operands = [left, right, lscale, rscale]
    aliases = {}
    if previous is not None:
        in_specs.append(pl.BlockSpec(memory_space=pl.ANY))
        operands.append(previous)
        aliases = {4: 0}
    size = 2 * own * groups * own * out_rows * LANES
    return pl.pallas_call(
        functools.partial(correlate_kernel, beams),
        grid=(groups,),
        in_specs=in_specs,
        out_specs=pl.BlockSpec(
            (2, 1, own, own, out_rows, LANES), lambda g: (0, index, 0, g, 0, 0)
        ),
        out_shape=jax.ShapeDtypeStruct(shape, jnp.float32),
        scratch_shapes=[
            pltpu.VMEM((polars, frames, rows, fine), jnp.float32),
            pltpu.VMEM((polars, frames, rows, fine), jnp.float32),
        ],
        input_output_aliases=aliases,
        compiler_params=pltpu.CompilerParams(vmem_limit_bytes=VMEM_LIMIT),
        cost_estimate=pl.CostEstimate(
            flops=size * 4 * frames * 100, bytes_accessed=size * 4, transcendentals=0
        ),
        name="correlate",
    )(*operands)


def routes(station_map, beam_index, own_count):
    block = station_map // own_count
    groups, dishes = station_map.shape
    order = jnp.arange(dishes, dtype=jnp.int32)
    same = block[:, :, None] == block[:, None, :]
    before = order[None, None, :] < order[None, :, None]
    rank = jnp.sum((same & before).astype(jnp.int32), axis=2)
    place = block * (dishes // groups) + rank
    hot = place[:, None, :] == order[None, :, None]
    station = jnp.sum(jnp.where(hot, station_map[:, None, :], 0), axis=2)
    row = jnp.sum(jnp.where(hot, beam_index[:, None, :], 0), axis=2)
    return hot, station, row


def per_device(voltages, fir_taps, station_map, beam_index, weight_table):
    components, coarse_dev, dishes_dev, frames_dev, polars, fine = voltages.shape
    history = fir_taps.shape[0] - 1
    table_rows, beams = weight_table.shape[1], weight_table.shape[3]
    groups = lax.axis_size("stn")
    own_count = STATIONS // groups
    share = dishes_dev // groups
    me = lax.axis_index("stn")
    earlier = shifted(voltages[:, :, :, frames_dev - history :], "tm", 1)
    table = dft_table(fine)
    both = lax.all_gather(jnp.stack([station_map, beam_index]), "stn")
    hot, station, row = routes(both[:, 0], both[:, 1], own_count)
    perm = lax.dynamic_index_in_dim(hot, me, 0, keepdims=False).astype(jnp.bfloat16)
    station = lax.dynamic_slice_in_dim(station, me * share, share, 1)
    row = lax.dynamic_slice_in_dim(row, me * share, share, 1)
    station_hot = (
        station[:, :, None] - me * own_count == jnp.arange(own_count, dtype=jnp.int32)
    ).astype(jnp.float32)
    table_hot = (row[:, :, None] == jnp.arange(table_rows, dtype=jnp.int32)).astype(jnp.bfloat16)
    weights = jnp.einsum(
        "gdt,otcb->ocgdb", table_hot, weight_table, preferred_element_type=jnp.float32
    )
    mixing = jnp.stack(
        [jnp.stack([weights[0], -weights[1]]), jnp.stack([weights[1], weights[0]])]
    )
    steering = jnp.einsum("gds,oicgdb->csobgid", station_hot, mixing).astype(jnp.bfloat16)
    steering = steering.reshape(coarse_dev, own_count * 2 * beams, groups * 2 * share)

    formed = []
    gathered = []
    power = 0.0
    spectra = []
    for c in range(coarse_dev):
        extended = jnp.concatenate([earlier[:, c], voltages[:, c]], axis=2)
        extended = jnp.transpose(extended, (3, 2, 0, 1, 4))
        terms = spectra_of(extended, fir_taps, table, perm, groups, frames_dev)
        if spectra:
            spectra[-1], terms = lax.optimization_barrier((spectra[-1], terms))
        spectra.append(lax.all_to_all(terms, "stn", 0, 0))
    for c in range(coarse_dev):
        values, squares = beams_of(spectra[c], steering[c])
        formed.append(values)
        gathered.append(lax.all_gather(values, "stn"))
        power = power + jnp.sum(squares.reshape(polars, own_count, 2, beams, fine), axis=(2, 4))
    power = lax.psum(power, "chan")
    inverse_rms = lax.rsqrt(power / (COARSE * frames_dev * fine) + epsilon)
    every = lax.all_gather(inverse_rms, "stn")
    lscale = jnp.broadcast_to(
        inverse_rms[..., None] / frames_dev, inverse_rms.shape + (LANES,)
    )
    rscale = jnp.broadcast_to(every[..., None], every.shape + (LANES,))
    result = None
    for c in range(coarse_dev):
        result = correlate(
            c, coarse_dev, beams, formed[c], gathered[c], lscale, rscale, result
        )
    halves = fine // LANES
    result = result.reshape(
        2, coarse_dev, own_count, STATIONS, beams, polars, halves, polars, LANES
    )
    result = jnp.swapaxes(result, 6, 7)
    return result.reshape(
        1, 2, coarse_dev, own_count, STATIONS, beams, polars, polars, fine
    )


def solution(mesh):
    in_specs = (
        P(None, "chan", "stn", "tm", None, None),
        P(),
        P("stn"),
        P("stn"),
        P(None, None, "chan", None),
    )
    out_specs = P("tm", None, "chan", "stn", None, None, None, None, None)
    return jax.shard_map(
        per_device, mesh=mesh, in_specs=in_specs, out_specs=out_specs, check_vma=False
    )
```

profile of v0, /device:TPU:0, one launch (start us, length us, event | category | flops | bytes accessed | tf_op | source)
XLA Modules:
  0.0 651.1 jit_solution(5279507947068555698)
XLA Ops:
  6.5 6.8 %slice.37 = bf16[2,2,128,15,2,256]{5,4,3,2,1,0:T(2,128)(2,1)S(1)} slice(bf16[2,2,128,16,2,256]{5,4,3,2,1,0:T(2,128)(2,1)} %param.5), slice={[0:2], [0:2], [0:128], [1:16], [0:2], [0:256]} | slice | bytes 15728640 | tf_op jit(solution)/shard_map/slice | solution.py:260
  13.3 0.0 copy-start.3
  13.3 0.0 copy-start.4
  13.3 4.9 copy.34
  18.3 5.5 collective-permute-start
  23.7 12.0 %all-gather.4 = s32[4,2,128]{2,1,0:T(2,128)S(1)} all-gather(s32[1,2,128]{2,1,0:T(2,128)S(1)} %add_bitcast_fusion), channel_id=2, replica_groups=mesh['tm'=2,'stn'=4,'chan'=4] {'stn'}, dimensions={0}, use_global_device_ids=true | all-gather | bytes 5120 | tf_op jit(solution)/shard_map/all_gather | solution.py:262
  35.8 0.2 convert_reduce_fusion
  36.1 0.6 fusion.8.perm_ref
  36.7 1.0 fusion.7
  37.7 1.1 sine_convert_fusion
  38.8 0.9 maximum_maximum_fusion.dft_ref
  39.7 8.6 %fusion.20 = (bf16[2,1,128,16,2,256]{5,4,3,2,1,0:T(2,128)(2,1)S(1)}, bf16[2,1,128,16,2,256]{5,4,3,2,1,0:T(2,128)(2,1)S(1)}) fusion(bf16[2,2,128,16,2,256]{5,4,3,2,1,0:T(2,128)(2,1)} %param.5), kind=kLoop, calls=%fused_computation.61 | loop fusion | bytes 16777216 | tf_op jit(solution)/shard_map/slice | solution.py:285
  48.3 11.4 %copy_bitcast_fusion = (bf16[2,128,16,2,256]{4,1,0,2,3:T(8,128)(2,1)}, bf16[2,128,16,2,256]{4,1,0,2,3:T(8,128)(2,1)}) fusion(bf16[2,1,128,16,2,256]{5,4,3,2,1,0:T(2,128)(2,1)S(1)} %get-tuple-element.19, bf16[2,1,128,16,2,256]{5,4,3,2,1,0:T(2,128)(2,1)S(1)} %get-tuple-element.20), kind=kLoop, calls=%fused_computation.2 | loop fusion | bytes 16777216 | tf_op jit(solution)/shard_map/squeeze | solution.py:285
  59.8 5.7 slice_bitcast_fusion
  65.4 7.4 %maximum_bitcast_fusion.x_ref = bf16[2,31,2,128,256]{4,3,2,1,0:T(8,128)(2,1)} fusion(bf16[2,128,16,2,256]{4,1,0,2,3:T(8,128)(2,1)} %get-tuple-element.35, bf16[2,128,15,2,256]{4,1,0,2,3:T(8,128)(2,1)} %get-tuple-element.22), kind=kLoop, calls=%fused_computation | loop fusion | flops 4063232 | bytes 16252928 | tf_op jit(solution)/shard_map/transpose | solution.py:286
  72.8 22.1 %spectra.2 = bf16[4,2,16,2,32,256]{5,4,3,2,1,0:T(8,128)(2,1)} custom-call(bf16[2,31,2,128,256]{4,3,2,1,0:T(8,128)(2,1)} %maximum_bitcast_fusion.x_ref, f32[16,256]{1,0:T(8,128)} %taps_ref.3, bf16[512,512]{1,0:T(8,128)(2,1)} %maximum_maximum_fusion.dft_ref, bf16[128,128]{1,0:T(8,128)(2,1)} %fusion.8.perm_ref), custom_call_target="tpu_custom_call" | custom-call | flops 10737418240 | bytes 16252928 | tf_op jit(solution)/shard_map/spectra/pallas_call | solution.py:76
  95.0 4.8 all-to-all-start
  99.8 0.2 all-gather.10.cloned.1.call-start
  100.0 0.2 select_reduce_fusion.1
  100.3 0.1 constant_dynamic-slice_fusion
  100.4 0.1 convolution_bitcast_fusion
  100.5 0.1 copy.27
  100.6 0.1 dynamic-slice_subtract_fusion
  100.7 0.5 fusion
  101.2 0.4 fusion.21
  101.6 0.8 squeeze.30.steer_ref
  102.5 7.4 %maximum_bitcast_fusion.1.x_ref = bf16[2,31,2,128,256]{4,3,2,1,0:T(8,128)(2,1)} fusion(bf16[2,128,16,2,256]{4,1,0,2,3:T(8,128)(2,1)} %get-tuple-element.34, bf16[2,128,15,2,256]{4,1,0,2,3:T(8,128)(2,1)} %get-tuple-element.21), kind=kLoop, calls=%fused_computation.1 | loop fusion | flops 4063232 | bytes 16252928 | tf_op jit(solution)/shard_map/transpose | solution.py:286
  109.9 22.1 %spectra.3 = bf16[4,2,16,2,32,256]{5,4,3,2,1,0:T(8,128)(2,1)} custom-call(bf16[2,31,2,128,256]{4,3,2,1,0:T(8,128)(2,1)} %maximum_bitcast_fusion.1.x_ref, f32[16,256]{1,0:T(8,128)} %taps_ref.3, bf16[512,512]{1,0:T(8,128)(2,1)} %maximum_maximum_fusion.dft_ref, bf16[128,128]{1,0:T(8,128)(2,1)} %fusion.8.perm_ref), custom_call_target="tpu_custom_call" | custom-call | flops 10737418240 | bytes 16252928 | tf_op jit(solution)/shard_map/spectra/pallas_call | solution.py:76
  132.0 55.8 %all-to-all-done.x_ref = bf16[4,2,16,2,32,256]{5,4,3,2,1,0:T(8,128)(2,1)} async-done(((bf16[4,2,16,2,32,256]{5,4,3,2,1,0:T(8,128)(2,1)}), bf16[4,2,16,2,32,256]{5,4,3,2,1,0:T(8,128)(2,1)}, u32[]{:S(2)}, u32[]{:S(2)}) %all-to-all-start) | async-done | bytes 4194336 | tf_op jit(solution)/shard_map/all_to_all | solution.py:290
  187.8 8.4 %beams.3 = (bf16[2,16,128,256]{3,2,1,0:T(8,128)(2,1)}, f32[2,128,256]{2,1,0:T(8,128)}) custom-call(bf16[4,2,16,2,32,256]{5,4,3,2,1,0:T(8,128)(2,1)} %all-to-all-done.x_ref, bf16[128,256]{1,0:T(8,128)(2,1)} %squeeze.30.steer_ref), custom_call_target="tpu_custom_call" | custom-call | flops 536870912 | bytes 8388608 | tf_op jit(solution)/shard_map/beams/pallas_call | solution.py:121
  196.1 0.0 all-gather.10.cloned.1.call-update
  196.2 4.9 all-to-all-start.1
  201.1 0.0 all-gather.8.cloned.1.call-start
  201.1 0.8 squeeze.29.steer_ref
  202.0 198.7 %all-to-all-done.1.x_ref = bf16[4,2,16,2,32,256]{5,4,3,2,1,0:T(8,128)(2,1)} async-done(((bf16[4,2,16,2,32,256]{5,4,3,2,1,0:T(8,128)(2,1)}), bf16[4,2,16,2,32,256]{5,4,3,2,1,0:T(8,128)(2,1)}, u32[]{:S(2)}, u32[]{:S(2)}) %all-to-all-start.1) | async-done | bytes 4194336 | tf_op jit(solution)/shard_map/all_to_all | solution.py:290
  400.7 8.3 %beams.2 = (bf16[2,16,128,256]{3,2,1,0:T(8,128)(2,1)}, f32[2,128,256]{2,1,0:T(8,128)}) custom-call(bf16[4,2,16,2,32,256]{5,4,3,2,1,0:T(8,128)(2,1)} %all-to-all-done.1.x_ref, bf16[128,256]{1,0:T(8,128)(2,1)} %squeeze.29.steer_ref), custom_call_target="tpu_custom_call" | custom-call | flops 536870912 | bytes 8388608 | tf_op jit(solution)/shard_map/beams/pallas_call | solution.py:121
  409.0 0.0 all-gather.8.cloned.1.call-update
  409.0 0.1 reduce_sum.65
  409.1 0.1 reduce_sum.66
  409.2 1.1 reduce_sum.68
  410.3 0.1 reduce_sum.69
  410.5 10.1 %psum.7 = f32[2,8,8]{2,1,0:T(8,128)S(1)} all-reduce(f32[2,8,8]{2,1,0:T(8,128)S(1)} %add.46), channel_id=1, replica_groups=mesh['tm'=2,'stn'=4,'chan'=4] {'chan'}, use_global_device_ids=true, to_apply=%region_7.8 | all-reduce | flops 128 | bytes 1024 | tf_op jit(solution)/shard_map/psum | solution.py:296
  420.5 15.3 %all-gather.2 = f32[8,8,8]{2,1,0:T(8,128)S(1)} all-gather(f32[2,8,8]{2,1,0:T(8,128)S(1)} %get-tuple-element.30), channel_id=4, replica_groups=mesh['tm'=2,'stn'=4,'chan'=4] {'stn'}, dimensions={0}, use_global_device_ids=true | all-gather | bytes 2560 | tf_op jit(solution)/shard_map/all_gather | solution.py:298
  435.8 0.7 broadcast_in_dim.48.lscale_ref
  436.5 0.8 broadcast_in_dim.49.rscale_ref
  437.4 65.2 %correlate.2.rest_0_ = f32[2,2,8,32,64,128]{5,4,3,2,1,0:T(8,128)} custom-call(bf16[2,16,128,256]{3,2,1,0:T(8,128)(2,1)} %get-tuple-element.16.left_ref, bf16[4,2,16,128,256]{4,3,2,1,0:T(8,128)(2,1)} %bitcast.64, f32[2,8,8,128]{3,2,1,0:T(8,128)} %broadcast_in_dim.48.lscale_ref, f32[4,2,8,8,128]{4,3,2,1,0:T(8,128)} %broadcast_in_dim.49.rscale_ref), custom_call_target="tpu_custom_call" | custom-call | flops 26843545600 | bytes 16777216 | tf_op jit(solution)/shard_map/correlate/pallas_call | solution.py:217
  502.5 77.1 %all-gather.8.cloned.1.call-done = bf16[8,16,128,256]{3,2,1,0:T(8,128)(2,1)} async-done(((bf16[2,16,128,256]{3,2,1,0:T(8,128)(2,1)}), bf16[8,16,128,256]{3,2,1,0:T(8,128)(2,1)}) %all-gather.8.cloned.1.call-update) | async-done | bytes 8388624 | tf_op jit(solution)/shard_map/all_gather | solution.py:294
  579.7 64.5 %correlate.3 = f32[2,2,8,32,64,128]{5,4,3,2,1,0:T(8,128)} custom-call(bf16[2,16,128,256]{3,2,1,0:T(8,128)(2,1)} %get-tuple-element.12.left_ref, bf16[4,2,16,128,256]{4,3,2,1,0:T(8,128)(2,1)} %bitcast.65, f32[2,8,8,128]{3,2,1,0:T(8,128)} %broadcast_in_dim.48.lscale_ref, ...), custom_call_target="tpu_custom_call", output_to_operand_aliasing={{}: (4, {})} | custom-call | flops 26843545600 | bytes 16777216 | tf_op jit(solution)/shard_map/correlate/pallas_call | solution.py:217
  (25 shorter events, 0.2 us)
Async XLA Ops:
  6.5 93.8 %copy-start = (bf16[2,16,2,8]{1,3,2,0:T(8,128)(2,1)S(1)}, bf16[2,16,2,8]{1,3,2,0:T(8,128)(2,1)}, u32[]{:S(2)}) copy-start(bf16[2,16,2,8]{1,3,2,0:T(8,128)(2,1)} %param.9) | copy-start | bytes 3076
  13.3 10.4 %copy-start.3 = (s32[128]{0:T(128)S(1)}, s32[128]{0:T(128)}, u32[]{:S(2)}) copy-start(s32[128]{0:T(128)} %param.8) | copy-start | bytes 1540
  13.3 10.4 %copy-start.4 = (s32[128]{0:T(128)S(1)}, s32[128]{0:T(128)}, u32[]{:S(2)}) copy-start(s32[128]{0:T(128)} %param.7) | copy-start | bytes 1540
  18.3 41.5 %collective-permute-start = (bf16[2,2,128,15,2,256]{5,2,0,3,4,1:T(8,128)(2,1)}, bf16[2,2,128,15,2,256]{5,2,0,3,4,1:T(8,128)(2,1)}, u32[]{:S(2)}, u32[]{:S(2)}) collective-permute-start(bf16[2,2,128,15,2,256]{5,2,0,3,4,1:T(8,128)(2,1)} %copy.34), channel_id=1, source_target_pairs={{0,16},{1,17},{2,18},{3,19},{4,20},{5,21},{6,22},{7,23},{8,24},{9,... | collective-permute-start | bytes 23592968 | tf_op jit(solution)/shard_map/ppermute | solution.py:21
  95.0 92.8 %all-to-all-start = ((bf16[4,2,16,2,32,256]{5,4,3,2,1,0:T(8,128)(2,1)}), bf16[4,2,16,2,32,256]{5,4,3,2,1,0:T(8,128)(2,1)}, u32[]{:S(2)}, u32[]{:S(2)}) async-start(bf16[4,2,16,2,32,256]{5,4,3,2,1,0:T(8,128)(2,1)} %spectra.2), calls=%async_computation | async-start | bytes 8388608 | tf_op jit(solution)/shard_map/all_to_all | solution.py:290
  99.8 336.0 %all-gather.10.cloned.1.call-start = ((), (), s32[]{:S(2)}) async-start(), calls=%async_computation.3 | async-start | bytes 10485760 | tf_op jit(solution)/shard_map/all_gather | solution.py:294
  196.2 204.5 %all-to-all-start.1 = ((bf16[4,2,16,2,32,256]{5,4,3,2,1,0:T(8,128)(2,1)}), bf16[4,2,16,2,32,256]{5,4,3,2,1,0:T(8,128)(2,1)}, u32[]{:S(2)}, u32[]{:S(2)}) async-start(bf16[4,2,16,2,32,256]{5,4,3,2,1,0:T(8,128)(2,1)} %spectra.3), calls=%async_computation.1 | async-start | bytes 8388608 | tf_op jit(solution)/shard_map/all_to_all | solution.py:290
  201.1 207.9 %copy-start.2 = (f32[2,128,256]{2,1,0:T(8,128)S(1)}, f32[2,128,256]{2,1,0:T(8,128)}, u32[]{:S(2)}) copy-start(f32[2,128,256]{2,1,0:T(8,128)} %get-tuple-element.14) | copy-start | bytes 786436
  201.1 378.6 %all-gather.8.cloned.1.call-start = ((), (), s32[]{:S(2)}) async-start(), calls=%async_computation.2 | async-start | bytes 10485760 | tf_op jit(solution)/shard_map/all_gather | solution.py:294
  579.7 64.5 %copy-start.1 = (bf16[2,16,2,8]{1,3,2,0:T(8,128)(2,1)S(1)}, bf16[2,16,2,8]{1,3,2,0:T(8,128)(2,1)}, u32[]{:S(2)}) copy-start(bf16[2,16,2,8]{1,3,2,0:T(8,128)(2,1)} %param.9) | copy-start | bytes 3076
Sparse Core Ops, SparseCore 0:
  196.3 233.0 all-gather.9
  431.0 148.6 all-gather.7
where the time goes:
time: 651 us
  waiting for transfers between devices  332 us (51%)
  Pallas kernels  191 us (29%)
  local copies, waits for them, and re-layouts  41.4 us (6%)
  blocking collectives  37.3 us (6%)
  other arithmetic  20.8 us (3%)
  starting transfers between devices  15.5 us (2%)
  between operations  13.6 us (2%)
    all_to_all x2, waiting for transfers between devices, per_device(): spectra.append(lax.all_to_all(terms, 'stn', 0, 0))  254 us
    pallas_call x2, Pallas kernels, correlate(): pl.pallas_call(functools.partial(correlate_kernel, beams), grid=(groups,)...  130 us
    all_gather x2, waiting for transfers between devices, per_device(): gathered.append(lax.all_gather(values, 'stn'))  77.1 us
    pallas_call x2, Pallas kernels, spectra_of(): pl.pallas_call(functools.partial(spectra_kernel, n_dest), grid=(polars,),...  44.3 us
    squeeze x2, local copies, waits for them, and re-layouts, per_device(): extended = jnp.concatenate([earlier[:, c], voltages[:, c]], axis=2)  17.1 us
    pallas_call x2, Pallas kernels, beams_of(): pl.pallas_call(beams_kernel, grid=(polars,), in_specs=[pl.BlockSpec((grou...  16.7 us
    all_gather x1, blocking collectives, per_device(): every = lax.all_gather(inverse_rms, 'stn')  15.3 us
    transpose x2, other arithmetic, per_device(): extended = jnp.transpose(extended, (3, 2, 0, 1, 4))  14.8 us
  transfers between devices with their start and end apart: 5, of which 3 were waited for; matrix products, arithmetic and copies ran while one was open for 6% of the time, Pallas kernels for 15%

commit v1 on v0

v1 whole, which is shorter than its diff:
```python
import functools

import jax
import jax.numpy as jnp
from jax import lax
from jax.experimental import pallas as pl
from jax.experimental.pallas import tpu as pltpu
from jax.sharding import PartitionSpec as P

LANES = 128
VMEM_LIMIT = 63 * 1024 * 1024
MESH = pl.DeviceIdType.MESH

epsilon = 1e-06


def dft_table(length):
    bin_index = jnp.arange(length, dtype=jnp.int32)
    phase_step = bin_index[:, None] * bin_index[None, :] % length
    angles = phase_step.astype(jnp.float32) * (2.0 * jnp.pi / length)
    cosine = jnp.cos(angles).astype(jnp.bfloat16)
    sine = jnp.sin(angles).astype(jnp.bfloat16)
    top = jnp.concatenate([cosine, -sine], axis=1)
    return jnp.concatenate([top, jnp.concatenate([sine, cosine], axis=1)], axis=0)


def chain_kernel(
    beams, volts, perm, steer, taps, dft, out,
    xin, send, recv, srecv, sfull, ybuf, fil, gbuf, pacc, pwx, scales, left, right, stage,
    load_sem, a_send, a_recv, s_send, s_recv, h_send, h_recv,
    b_send, b_recv, p_send, p_recv, c_send, c_recv, o_sem,
):
    coarse, polars, frames, _, dishes, fine = volts.shape
    chunks = coarse * polars
    n_taps = taps.shape[0]
    history = n_taps - 1
    n = lax.axis_size("stn")
    n_tm = lax.axis_size("tm")
    n_chan = lax.axis_size("chan")
    me = lax.axis_index("stn")
    tm = lax.axis_index("tm")
    ch = lax.axis_index("chan")
    share = dishes // n
    rows = sfull.shape[1]
    half_rows = rows // 2
    own = half_rows // beams
    halves = fine // LANES
    group = 4

    barrier = pltpu.get_barrier_semaphore()
    for k in range(1, n):
        pl.semaphore_signal(
            barrier, inc=1, device_id={"stn": lax.rem(me + k, n)}, device_id_type=MESH
        )
    for k in range(1, n_chan):
        pl.semaphore_signal(
            barrier, inc=1, device_id={"chan": lax.rem(ch + k, n_chan)}, device_id_type=MESH
        )
    for k in range(1, n_tm):
        pl.semaphore_signal(
            barrier, inc=1, device_id={"tm": lax.rem(tm + k, n_tm)}, device_id_type=MESH
        )

    def load(chunk):
        return pltpu.make_async_copy(
            volts.at[chunk // polars, chunk % polars],
            xin.at[chunk % 2],
            load_sem.at[chunk % 2],
        )

    def steer_copy(k):
        dest = lax.rem(me + k, n)
        return pltpu.make_async_remote_copy(
            src_ref=steer.at[dest], dst_ref=srecv.at[me],
            send_sem=s_send.at[k - 1], recv_sem=s_recv.at[k - 1],
            device_id={"stn": dest}, device_id_type=MESH,
        )

    def steer_arrival(k):
        return pltpu.make_async_remote_copy(
            src_ref=steer.at[me], dst_ref=srecv.at[lax.rem(me + n - k, n)],
            send_sem=s_send.at[k - 1], recv_sem=s_recv.at[k - 1],
            device_id={"stn": lax.rem(me + k, n)}, device_id_type=MESH,
        )

    def dish_copy(chunk, k):
        dest = lax.rem(me + k, n)
        return pltpu.make_async_remote_copy(
            src_ref=send.at[chunk, dest], dst_ref=recv.at[chunk, me],
            send_sem=a_send.at[chunk, k - 1], recv_sem=a_recv.at[chunk, k - 1],
            device_id={"stn": dest}, device_id_type=MESH,
        )

    def dish_arrival(chunk, k):
        return pltpu.make_async_remote_copy(
            src_ref=send.at[chunk, me], dst_ref=recv.at[chunk, lax.rem(me + n - k, n)],
            send_sem=a_send.at[chunk, k - 1], recv_sem=a_recv.at[chunk, k - 1],
            device_id={"stn": lax.rem(me + k, n)}, device_id_type=MESH,
        )

    load(0).start()
    srecv[me] = steer[me]

    for chunk in range(chunks):
        load(chunk).wait()
        if chunk + 1 < chunks:
            load(chunk + 1).start()

        def sort_step(i, carry):
            frame = i // 2
            o = i % 2
            moved = jnp.dot(
                perm[...], xin[chunk % 2, frame, o], preferred_element_type=jnp.float32
            ).astype(jnp.bfloat16)
            for dest in range(n):
                send[chunk, dest, frame, o] = moved[dest * share : (dest + 1) * share]
            return carry

        lax.fori_loop(0, 2 * frames, sort_step, 0)
        if chunk == 0:
            pl.semaphore_wait(barrier, (n - 1) + (n_chan - 1) + (n_tm - 1))
            for k in range(1, n):
                steer_copy(k).start()
        for k in range(1, n):
            dish_copy(chunk, k).start()

    def keep_step(i, carry):
        for chunk in range(chunks):
            recv[chunk, me, i] = send[chunk, me, i]
        return carry

    lax.fori_loop(0, frames, keep_step, 0)

    @pl.when(tm == 0)
    def _():
        def zero_step(i, carry):
            for chunk in range(chunks):
                ybuf[chunk, i] = jnp.zeros((rows, fine), jnp.bfloat16)
            return carry

        lax.fori_loop(0, history, zero_step, 0)

    pacc[...] = jnp.zeros_like(pacc)

    for k in range(1, n):
        steer_arrival(k).wait_recv()
    for c in range(coarse):
        columns = srecv[:, c].astype(jnp.float32).reshape(n * 2 * share, rows)
        sfull[c] = jnp.transpose(columns).astype(jnp.bfloat16)

    def halo(chunk):
        return pltpu.make_async_remote_copy(
            src_ref=ybuf.at[chunk, pl.ds(frames, history)],
            dst_ref=ybuf.at[chunk, pl.ds(0, history)],
            send_sem=h_send.at[chunk], recv_sem=h_recv.at[chunk],
            device_id={"tm": lax.rem(tm + 1, n_tm)}, device_id_type=MESH,
        )

    def beam_copy(block, chunk, right_way, distance):
        target = me + 1 if right_way else me - 1
        way = 0 if right_way else 1
        return pltpu.make_async_remote_copy(
            src_ref=gbuf.at[block, chunk], dst_ref=gbuf.at[block, chunk],
            send_sem=b_send.at[way, distance, chunk], recv_sem=b_recv.at[way, distance, chunk],
            device_id={"stn": lax.rem(target + n, n)}, device_id_type=MESH,
        )

    def chunk_work(chunk):
        c, p = chunk // polars, chunk % polars
        for k in range(1, n):
            dish_arrival(chunk, k).wait_recv()

        def beam_step(frame, carry):
            terms = recv[chunk, :, frame]
            if share % 16:
                terms = terms.astype(jnp.float32).reshape(-1, fine).astype(jnp.bfloat16)
            else:
                terms = terms.reshape(-1, fine)
            formed = jnp.dot(sfull[c], terms, preferred_element_type=jnp.float32)
            ybuf[chunk, history + frame] = formed.astype(jnp.bfloat16)
            return carry

        lax.fori_loop(0, frames, beam_step, 0)

        @pl.when(tm < n_tm - 1)
        def _():
            halo(chunk).start()

        @pl.when(tm > 0)
        def _():
            halo(chunk).wait_recv()

        part = min(32, half_rows)

        def filter_step(i, carry):
            for j in range(group):
                frame = i * group + j
                for o in range(2):
                    for low in range(0, half_rows, part):
                        start = o * half_rows + low
                        total = jnp.zeros((part, fine), jnp.float32)
                        for tap in range(n_taps):
                            sample = ybuf[chunk, frame + (history - tap), start : start + part, :]
                            total = total + taps[tap : tap + 1, :] * sample.astype(jnp.float32)
                        fil[
                            j * half_rows + low : j * half_rows + low + part,
                            o * fine : (o + 1) * fine,
                        ] = total.astype(jnp.bfloat16)
            spec = jnp.dot(fil[...], dft[...], preferred_element_type=jnp.float32)
            spec = spec.astype(jnp.bfloat16)
            for j in range(group):
                for o in range(2):
                    values = spec[j * half_rows : (j + 1) * half_rows, o * fine : (o + 1) * fine]
                    gbuf[me, chunk, i * group + j, o * half_rows : (o + 1) * half_rows, :] = values
                    wide = values.astype(jnp.float32)
                    pacc[p] += wide * wide
            return carry

        lax.fori_loop(0, frames // group, filter_step, 0)

        @pl.when(me < n - 1)
        def _():
            beam_copy(me, chunk, True, 0).start()

        @pl.when(me > 0)
        def _():
            beam_copy(me, chunk, False, 0).start()

    inner = jnp.logical_and(me > 0, me < n - 1)

    def from_side(block, chunk, right_way, distance, forward):
        beam_copy(block, chunk, right_way, distance).wait_recv()
        if forward:
            beam_copy(block, chunk, right_way, distance + 1).start()

    def pass_on(distance, chunk):
        @pl.when(inner)
        def _():
            @pl.when(me - distance >= 0)
            def _():
                from_side(me - distance, chunk, True, distance - 1, True)

            @pl.when(me + distance < n)
            def _():
                from_side(me + distance, chunk, False, distance - 1, True)

    def arrive(distance, chunk):
        @pl.when(me == n - 1)
        def _():
            from_side(me - distance, chunk, True, distance - 1, False)

        @pl.when(me == 0)
        def _():
            from_side(me + distance, chunk, False, distance - 1, False)

    def power_copy(k):
        return pltpu.make_async_remote_copy(
            src_ref=pwx.at[ch], dst_ref=pwx.at[ch],
            send_sem=p_send.at[k - 1], recv_sem=p_recv.at[k - 1],
            device_id={"chan": lax.rem(ch + k, n_chan)}, device_id_type=MESH,
        )

    def power_arrival(k):
        other = lax.rem(ch + n_chan - k, n_chan)
        return pltpu.make_async_remote_copy(
            src_ref=pwx.at[ch], dst_ref=pwx.at[other],
            send_sem=p_send.at[k - 1], recv_sem=p_recv.at[k - 1],
            device_id={"chan": lax.rem(ch + k, n_chan)}, device_id_type=MESH,
        )

    def scale_copy(k):
        return pltpu.make_async_remote_copy(
            src_ref=scales.at[me], dst_ref=scales.at[me],
            send_sem=c_send.at[k - 1], recv_sem=c_recv.at[k - 1],
            device_id={"stn": lax.rem(me + k, n)}, device_id_type=MESH,
        )

    def scale_arrival(k):
        other = lax.rem(me + n - k, n)
        return pltpu.make_async_remote_copy(
            src_ref=scales.at[me], dst_ref=scales.at[other],
            send_sem=c_send.at[k - 1], recv_sem=c_recv.at[k - 1],
            device_id={"stn": lax.rem(me + k, n)}, device_id_type=MESH,
        )

    def power_work():
        for p in range(polars):
            total = jnp.sum(pacc[p], axis=1, keepdims=True)
            pwx[ch, p] = jnp.broadcast_to(total, (half_rows, LANES))
        for k in range(1, n_chan):
            power_copy(k).start()
        for k in range(1, n_chan):
            power_arrival(k).wait_recv()
        total = pwx[0]
        for k in range(1, n_chan):
            total = total + pwx[k]
        scales[me] = lax.rsqrt(total / (coarse * n_chan * frames * fine) + epsilon)
        for k in range(1, n):
            scale_copy(k).start()
        for k in range(1, n):
            scale_arrival(k).wait_recv()

    def widen(block, c, target):
        def step(i, carry):
            for p in range(polars):
                target[p, i] = gbuf[block, c * polars + p, i].astype(jnp.float32)
            return carry

        lax.fori_loop(0, frames, step, 0)

    def out_copy(slot, c, s, block):
        return pltpu.make_async_copy(
            stage.at[slot], out.at[:, c, s, pl.ds(block * own, own)], o_sem.at[slot]
        )

    def correlate(c, block, first):
        widen(block, c, right)

        def station(s, carry):
            slot = s % 2
            srow = pl.multiple_of(s * beams, beams)
            if first:
                @pl.when(s >= 2)
                def _():
                    out_copy(slot, c, s, block).wait()
            else:
                out_copy(slot, c, s, block).wait()

            def pair(t, inner_carry):
                trow = pl.multiple_of(t * beams, beams)
                for half in range(halves):
                    lanes = pl.ds(half * LANES, LANES)
                    re = {}
                    im = {}
                    for f in range(frames):
                        lre = [left[p, f, pl.ds(srow, beams), lanes] for p in range(polars)]
                        lim = [
                            left[p, f, pl.ds(half_rows + srow, beams), lanes]
                            for p in range(polars)
                        ]
                        rre = [right[q, f, pl.ds(trow, beams), lanes] for q in range(polars)]
                        rim = [
                            right[q, f, pl.ds(half_rows + trow, beams), lanes]
                            for q in range(polars)
                        ]
                        for p in range(polars):
                            for q in range(polars):
                                a = lre[p] * rre[q] + lim[p] * rim[q]
                                b = lim[p] * rre[q] - lre[p] * rim[q]
                                re[p, q] = a if f == 0 else re[p, q] + a
                                im[p, q] = b if f == 0 else im[p, q] + b
                    for p in range(polars):
                        for q in range(polars):
                            scale = (
                                scales[me, p, pl.ds(srow, beams), :]
                                * scales[block, q, pl.ds(trow, beams), :]
                                * (1.0 / frames)
                            )
                            row = (p * halves + half) * polars + q
                            where = pl.ds(row, beams, stride=polars * polars * halves)
                            stage[slot, 0, t, where, :] = re[p, q] * scale
                            stage[slot, 1, t, where, :] = im[p, q] * scale
                return inner_carry

            lax.fori_loop(0, own, pair, 0)
            out_copy(slot, c, s, block).start()
            return carry

        lax.fori_loop(0, own, station, 0)

    def order(step):
        if step == 0:
            return me
        two_sided = jnp.minimum(me, n - 1 - me)
        near = (step + 1) // 2
        near_block = me - near if step % 2 else me + near
        far = step - two_sided
        far_block = jnp.where(me < n - 1 - me, me + far, me - far)
        return jnp.where(step <= 2 * two_sided, near_block, far_block)

    for chunk in range(polars):
        chunk_work(chunk)
    for c in range(1, coarse):
        for p in range(polars):
            chunk_work(c * polars + p)
            for q in range(polars):
                if p == 0:
                    pass_on(1, (c - 1) * polars + q)
        for distance in range(2, n - 1):
            for q in range(polars):
                pass_on(distance, (c - 1) * polars + q)
    power_work()
    widen(me, 0, left)
    last = coarse - 1
    for c in range(coarse):
        if c:
            widen(me, c, left)
        for step in range(n):
            if step >= 1:
                for q in range(polars):
                    arrive(step, c * polars + q)
            if c == last and coarse == 1 and step == 0:
                for distance in range(1, n - 1):
                    for q in range(polars):
                        pass_on(distance, c * polars + q)
            correlate(c, order(step), c == 0 and step == 0)
            if c == last - 1 and step >= n - 2:
                for q in range(polars):
                    if step == n - 2:
                        pass_on(1, last * polars + q)
            if c == last - 1 and step == n - 1:
                for distance in range(2, n - 1):
                    for q in range(polars):
                        pass_on(distance, last * polars + q)

    for slot in range(2):
        out_copy(slot, last, own - 2 + slot, order(n - 1)).wait()
    for k in range(1, n):
        steer_copy(k).wait_send()
        scale_copy(k).wait_send()
        for chunk in range(chunks):
            dish_copy(chunk, k).wait_send()
    for k in range(1, n_chan):
        power_copy(k).wait_send()

    @pl.when(tm < n_tm - 1)
    def _():
        for chunk in range(chunks):
            halo(chunk).wait_send()

    for distance in range(n - 1):
        for chunk in range(chunks):
            @pl.when(jnp.logical_and(me - distance >= 0, me < n - 1))
            def _():
                beam_copy(me - distance, chunk, True, distance).wait_send()

            @pl.when(jnp.logical_and(me + distance < n, me > 0))
            def _():
                beam_copy(me + distance, chunk, False, distance).wait_send()


def chain(volts, perm, steer, fir_taps, table, beams):
    coarse, polars, frames, _, dishes, fine = volts.shape
    n, _, terms, rows = steer.shape
    n_chan = lax.axis_size("chan")
    share = dishes // n
    chunks = coarse * polars
    half_rows = rows // 2
    own = half_rows // beams
    out_rows = beams * polars * polars * (fine // LANES)
    history = fir_taps.shape[0] - 1
    dma = pltpu.SemaphoreType.DMA
    bf16, f32 = jnp.bfloat16, jnp.float32
    size = 2 * coarse * own * n * own * out_rows * LANES
    vmem = pl.BlockSpec(memory_space=pltpu.VMEM)
    return pl.pallas_call(
        functools.partial(chain_kernel, beams),
        in_specs=[pl.BlockSpec(memory_space=pl.ANY), vmem, vmem, vmem, vmem],
        out_specs=pl.BlockSpec(memory_space=pl.ANY),
        out_shape=jax.ShapeDtypeStruct((2, coarse, own, n * own, out_rows, LANES), f32),
        scratch_shapes=[
            pltpu.VMEM((2, frames, 2, dishes, fine), bf16),
            pltpu.VMEM((chunks, n, frames, 2, share, fine), bf16),
            pltpu.VMEM((chunks, n, frames, 2, share, fine), bf16),
            pltpu.VMEM((n, coarse, terms, rows), bf16),
            pltpu.VMEM((coarse, rows, n * terms), bf16),
            pltpu.VMEM((chunks, history + frames, rows, fine), bf16),
            pltpu.VMEM((4 * half_rows, 2 * fine), bf16),
            pltpu.VMEM((n, chunks, frames, rows, fine), bf16),
            pltpu.VMEM((polars, half_rows, fine), f32),
            pltpu.VMEM((n_chan, polars, half_rows, LANES), f32),
            pltpu.VMEM((n, polars, half_rows, LANES), f32),
            pltpu.VMEM((polars, frames, rows, fine), f32),
            pltpu.VMEM((polars, frames, rows, fine), f32),
            pltpu.VMEM((2, 2, own, out_rows, LANES), f32),
            dma((2,)),
            dma((chunks, n - 1)),
            dma((chunks, n - 1)),
            dma((n - 1,)),
            dma((n - 1,)),
            dma((chunks,)),
            dma((chunks,)),
            dma((2, n - 1, chunks)),
            dma((2, n - 1, chunks)),
            dma((n_chan - 1,)),
            dma((n_chan - 1,)),
            dma((n - 1,)),
            dma((n - 1,)),
            dma((2,)),
        ],
        compiler_params=pltpu.CompilerParams(
            vmem_limit_bytes=VMEM_LIMIT, collective_id=0, has_side_effects=True
        ),
        cost_estimate=pl.CostEstimate(
            flops=size * 4 * frames * 100, bytes_accessed=size * 4, transcendentals=0
        ),
        name="chain",
    )(volts, perm, steer, fir_taps, table)


def per_device(voltages, fir_taps, station_map, beam_index, weight_table):
    _, coarse_dev, dishes, frames, polars, fine = voltages.shape
    table_rows, beams = weight_table.shape[1], weight_table.shape[3]
    n = lax.axis_size("stn")
    share = dishes // n
    total_stations = 32
    own = total_stations // n
    order = jnp.arange(dishes, dtype=jnp.int32)
    block = station_map // own
    same = block[:, None] == block[None, :]
    before = order[None, :] < order[:, None]
    rank = jnp.sum((same & before).astype(jnp.int32), axis=1)
    place = block * share + rank
    hot = place[None, :] == order[:, None]
    perm = hot.astype(jnp.bfloat16)
    station = jnp.sum(jnp.where(hot, (station_map - block * own)[None, :], 0), axis=1)
    row = jnp.sum(jnp.where(hot, beam_index[None, :], 0), axis=1)
    station_hot = station[:, None] == jnp.arange(own, dtype=jnp.int32)
    table_hot = (row[:, None] == jnp.arange(table_rows, dtype=jnp.int32)).astype(jnp.bfloat16)
    weights = jnp.einsum(
        "dt,otcb->ocdb", table_hot, weight_table, preferred_element_type=jnp.float32
    ).astype(jnp.bfloat16)
    mixing = jnp.stack(
        [jnp.stack([weights[0], weights[1]]), jnp.stack([-weights[1], weights[0]])]
    )
    mixing = mixing.reshape(2, 2, coarse_dev, n, share, 1, beams)
    steer = jnp.where(
        station_hot.reshape(1, 1, 1, n, share, own, 1), mixing, jnp.zeros((), jnp.bfloat16)
    )
    steer = jnp.transpose(steer, (3, 2, 0, 4, 1, 5, 6))
    steer = steer.reshape(n, coarse_dev, 2 * share, 2 * own * beams)
    volts = jnp.transpose(voltages, (1, 4, 3, 0, 2, 5))
    result = chain(volts, perm, steer, fir_taps, dft_table(fine), beams)
    halves = fine // LANES
    result = result.reshape(
        2, coarse_dev, own, total_stations, beams, polars, halves, polars, LANES
    )
    result = jnp.swapaxes(result, 6, 7)
    return result.reshape(1, 2, coarse_dev, own, total_stations, beams, polars, polars, fine)


def solution(mesh):
    in_specs = (
        P(None, "chan", "stn", "tm", None, None),
        P(),
        P("stn"),
        P("stn"),
        P(None, None, "chan", None),
    )
    out_specs = P("tm", None, "chan", "stn", None, None, None, None, None)
    return jax.shard_map(
        per_device, mesh=mesh, in_specs=in_specs, out_specs=out_specs, check_vma=False
    )
```

time: 651 us -> 532 us (0.82)
  waiting for transfers between devices: 332 us -> 0 us
  Pallas kernels: 191 us -> 489 us
  blocking collectives: 37.3 us -> 0 us
  starting transfers between devices: 15.5 us -> 0 us
  other arithmetic: 20.8 us -> 5.87 us
  between operations: 13.6 us -> 0.27 us
    pallas_call x6 -> x1, Pallas kernels: 191 us -> 489 us  [chain(): pl.pallas_call(functools.partial(chain_kernel, beams), in_specs=[pl.Block...]
    all_to_all x2 -> x0, waiting for transfers between devices: 254 us -> none  [per_device(): spectra.append(lax.all_to_all(terms, 'stn', 0, 0))]
    all_gather x2 -> x0, waiting for transfers between devices: 77.1 us -> none  [per_device(): gathered.append(lax.all_gather(values, 'stn'))]
    unnamed x11 -> x6, local copies, waits for them, and re-layouts: 4.95 us -> 34.9 us
    all_gather x2 -> x0, blocking collectives: 27.3 us -> none  [the longest x1 15.3 us: per_device(): every = lax.all_gather(inverse_rms, 'stn')]
    squeeze x4 -> x0, local copies, waits for them, and re-layouts: 18.8 us -> none  [the longest x2 17.1 us: per_device(): extended = jnp.concatenate([earlier[:, c], voltages[:, c]], axis=2)]
    slice x4 -> x0, local copies, waits for them, and re-layouts: 15.8 us -> none  [the longest x1 8.61 us: per_device(): extended = jnp.concatenate([earlier[:, c], voltages[:, c]], axis=2)]
    transpose x2 -> x0, other arithmetic: 14.8 us -> none  [per_device(): extended = jnp.transpose(extended, (3, 2, 0, 1, 4))]
  transfers between devices with their start and end apart: 5 -> 0, of which waited for: 3 -> 0; matrix products, arithmetic and copies ran while one was open for 6% -> 0% of each run, Pallas kernels for 15% -> 0%
where the time goes in v1:
time: 532 us
  Pallas kernels  489 us (92%)
  local copies, waits for them, and re-layouts  36.4 us (7%)
  other arithmetic  5.87 us (1%)
    pallas_call x1, Pallas kernels, chain(): pl.pallas_call(functools.partial(chain_kernel, beams), in_specs=[pl.Block...  489 us
    unnamed x6, local copies, waits for them, and re-layouts  34.9 us

profile of v1, /device:TPU:0, one launch (start us, length us, event | category | flops | bytes accessed | tf_op | source)
XLA Modules:
  0.0 532.0 jit_solution(7396971909641582611)
XLA Ops:
  0.0 0.0 copy-start
  0.0 0.7 copy-done
  0.7 0.7 multiply_subtract_fusion
  1.4 0.2 convert_reduce_fusion
  1.5 0.8 select_reduce_fusion.1
  2.3 0.1 eq.63
  2.4 0.1 fusion.9
  2.6 0.1 stack.16
  2.7 0.1 stack.14
  2.7 0.1 maximum_bitcast_fusion
  2.8 0.1 copy.16
  2.9 0.6 fusion.6.perm
  3.5 1.0 fusion.8
  4.5 0.1 broadcast_in_dim.64
  4.6 0.2 broadcast_in_dim.65
  4.9 0.1 copy.15
  5.0 1.1 sine_convert_fusion
  6.1 0.8 maximum_maximum_fusion.dft
  6.9 0.3 broadcast_in_dim.70
  7.2 0.3 broadcast_in_dim.71
  7.5 0.1 copy.17
  7.6 0.7 broadcast_select_fusion.steer
  8.3 11.6 %copy.20 = bf16[2,2,128,16,2,256]{5,2,0,3,4,1:T(8,128)(2,1)} copy(bf16[2,2,128,16,2,256]{5,4,3,2,1,0:T(2,128)(2,1)} %param.5) | data formatting | bytes 16777216 | tf_op args[0]
  19.9 489.3 %chain.1 = f32[2,2,8,32,64,128]{5,4,3,2,1,0:T(8,128)} custom-call(bf16[2,2,16,2,128,256]{5,4,3,2,1,0:T(8,128)(2,1)} %bitcast.33, bf16[128,128]{1,0:T(8,128)(2,1)} %fusion.6.perm, bf16[4,2,64,128]{3,2,1,0:T(8,128)(2,1)} %broadcast_select_fusion.steer, f32[16,256]{1,0:T(8,128)} %taps.1, bf16[512,512]{1,0:T(8,128)(2,1)} %maximum_maximum_fusion.dft), custom_call_target="tpu_custom_call" | custom-call | flops 53687091200 | bytes 33554432 | tf_op jit(solution)/shard_map/chain/pallas_call | solution.py:456
  509.2 0.0 copy-start.1
  509.2 22.7 %copy.22 = f32[1,2,2,8,32,8,2,2,256]{8,7,6,5,4,3,2,1,0:T(2,128)} copy(f32[1,2,2,8,32,8,2,2,256]{8,7,6,5,4,3,2,1,0:T(2,128)} %bitcast.32) | data formatting | bytes 67108864
  531.8 0.0 copy-done.1
  (5 shorter events, 0.0 us)
Async XLA Ops:
  0.0 0.7 copy-start
  509.2 22.7 %copy-start.1 = (bf16[2,16,2,8]{1,3,2,0:T(8,128)(2,1)S(1)}, bf16[2,16,2,8]{1,3,2,0:T(8,128)(2,1)}, u32[]{:S(2)}) copy-start(bf16[2,16,2,8]{1,3,2,0:T(8,128)(2,1)} %param.9) | copy-start | bytes 3076

commit v2 on v1

--- a/solution.py
+++ b/solution.py
@@ -2,6 +2,7 @@
 
 import jax
 import jax.numpy as jnp
+import numpy as np
 from jax import lax
 from jax.experimental import pallas as pl
 from jax.experimental.pallas import tpu as pltpu
@@ -15,20 +16,20 @@
 
 
 def dft_table(length):
-    bin_index = jnp.arange(length, dtype=jnp.int32)
+    bin_index = np.arange(length)
     phase_step = bin_index[:, None] * bin_index[None, :] % length
-    angles = phase_step.astype(jnp.float32) * (2.0 * jnp.pi / length)
-    cosine = jnp.cos(angles).astype(jnp.bfloat16)
-    sine = jnp.sin(angles).astype(jnp.bfloat16)
-    top = jnp.concatenate([cosine, -sine], axis=1)
-    return jnp.concatenate([top, jnp.concatenate([sine, cosine], axis=1)], axis=0)
+    angles = (2.0 * np.pi / length) * phase_step
+    cosine = np.cos(angles)
+    sine = np.sin(angles)
+    table = np.block([[cosine, -sine], [sine, cosine]])
+    return jnp.asarray(table.astype(np.float32), jnp.bfloat16)
 
 
 def chain_kernel(
-    beams, volts, perm, steer, taps, dft, out,
-    xin, send, recv, srecv, sfull, ybuf, fil, gbuf, pacc, pwx, scales, left, right, stage,
+    beams, volts, perm, steer, taps, dft, out, lout, rout,
+    xin, send, recv, srecv, sfull, ybuf, fil, gbuf, pacc, pwx, scales, lrows, rrows, left, right, stage,
     load_sem, a_send, a_recv, s_send, s_recv, h_send, h_recv,
-    b_send, b_recv, p_send, p_recv, c_send, c_recv, o_sem,
+    b_send, b_recv, p_send, p_recv, c_send, c_recv, o_sem, r_sem,
 ):
     coarse, polars, frames, _, dishes, fine = volts.shape
     chunks = coarse * polars
@@ -46,6 +47,8 @@
     own = half_rows // beams
     halves = fine // LANES
     group = 4
+    unroll = 8
+    ahead = 2
 
     barrier = pltpu.get_barrier_semaphore()
     for k in range(1, n):
@@ -97,6 +100,16 @@
             send_sem=a_send.at[chunk, k - 1], recv_sem=a_recv.at[chunk, k - 1],
             device_id={"stn": lax.rem(me + k, n)}, device_id_type=MESH,
         )
+
+    def send_dishes(chunk):
+        for distance in range(1, n):
+            @pl.when(me + distance < n)
+            def _():
+                dish_copy(chunk, distance).start()
+
+            @pl.when(me - distance >= 0)
+            def _():
+                dish_copy(chunk, n - distance).start()
 
     load(0).start()
     srecv[me] = steer[me]
@@ -121,8 +134,8 @@
             pl.semaphore_wait(barrier, (n - 1) + (n_chan - 1) + (n_tm - 1))
             for k in range(1, n):
                 steer_copy(k).start()
-        for k in range(1, n):
-            dish_copy(chunk, k).start()
+        if chunk < ahead:
+            send_dishes(chunk)
 
     def keep_step(i, carry):
         for chunk in range(chunks):
@@ -165,10 +178,44 @@
             device_id={"stn": lax.rem(target + n, n)}, device_id_type=MESH,
         )
 
+    inner = jnp.logical_and(me > 0, me < n - 1)
+    low_side = me < n - 1 - me
+
+    def on_side(far_way, distance, chunk, hop, act):
+        for right_way in (True, False):
+            block = me - distance if right_way else me + distance
+            inside = block >= 0 if right_way else block < n
+            side = low_side if right_way == far_way else jnp.logical_not(low_side)
+
+            @pl.when(jnp.logical_and(jnp.logical_and(inner, side), inside))
+            def _():
+                act(beam_copy(block, chunk, right_way, hop))
+
+    outward = (True, 2, [])
+    inward_end = (False, 5, [])
+
+    def launch(queue, distance, chunk):
+        far_way, window, started = queue
+        if len(started) >= window:
+            past, past_chunk = started[-window]
+            on_side(far_way, past, past_chunk, past, lambda copy: copy.wait_send())
+        started.append((distance, chunk))
+        on_side(far_way, distance, chunk, distance, lambda copy: copy.start())
+
+    def receive(queue, distance, chunk):
+        on_side(queue[0], distance, chunk, distance - 1, lambda copy: copy.wait_recv())
+
+    def drain(queue):
+        far_way, window, started = queue
+        for distance, chunk in started[-window:]:
+            on_side(far_way, distance, chunk, distance, lambda copy: copy.wait_send())
+
     def chunk_work(chunk):
         c, p = chunk // polars, chunk % polars
         for k in range(1, n):
             dish_arrival(chunk, k).wait_recv()
+        if chunk + ahead < chunks:
+            send_dishes(chunk + ahead)
 
         def beam_step(frame, carry):
             terms = recv[chunk, :, frame]
@@ -218,40 +265,24 @@
 
         lax.fori_loop(0, frames // group, filter_step, 0)
 
-        @pl.when(me < n - 1)
+        @pl.when(me == 0)
         def _():
             beam_copy(me, chunk, True, 0).start()
 
-        @pl.when(me > 0)
+        @pl.when(me == n - 1)
         def _():
             beam_copy(me, chunk, False, 0).start()
 
-    inner = jnp.logical_and(me > 0, me < n - 1)
-
-    def from_side(block, chunk, right_way, distance, forward):
-        beam_copy(block, chunk, right_way, distance).wait_recv()
-        if forward:
-            beam_copy(block, chunk, right_way, distance + 1).start()
-
-    def pass_on(distance, chunk):
-        @pl.when(inner)
-        def _():
-            @pl.when(me - distance >= 0)
-            def _():
-                from_side(me - distance, chunk, True, distance - 1, True)
-
-            @pl.when(me + distance < n)
-            def _():
-                from_side(me + distance, chunk, False, distance - 1, True)
+        launch(inward_end, 0, chunk)
 
     def arrive(distance, chunk):
         @pl.when(me == n - 1)
         def _():
-            from_side(me - distance, chunk, True, distance - 1, False)
+            beam_copy(me - distance, chunk, True, distance - 1).wait_recv()
 
         @pl.when(me == 0)
         def _():
-            from_side(me + distance, chunk, False, distance - 1, False)
+            beam_copy(me + distance, chunk, False, distance - 1).wait_recv()
 
     def power_copy(k):
         return pltpu.make_async_remote_copy(
@@ -283,12 +314,14 @@
             device_id={"stn": lax.rem(me + k, n)}, device_id_type=MESH,
         )
 
-    def power_work():
+    def power_start():
         for p in range(polars):
             total = jnp.sum(pacc[p], axis=1, keepdims=True)
             pwx[ch, p] = jnp.broadcast_to(total, (half_rows, LANES))
         for k in range(1, n_chan):
             power_copy(k).start()
+
+    def power_finish():
         for k in range(1, n_chan):
             power_arrival(k).wait_recv()
         total = pwx[0]
@@ -297,8 +330,41 @@
         scales[me] = lax.rsqrt(total / (coarse * n_chan * frames * fine) + epsilon)
         for k in range(1, n):
             scale_copy(k).start()
+
+    def row_copies():
+        return (
+            pltpu.make_async_copy(lrows, lout, r_sem.at[0]),
+            pltpu.make_async_copy(rrows, rout, r_sem.at[1]),
+        )
+
+    def scale_rows():
         for k in range(1, n):
             scale_arrival(k).wait_recv()
+
+        def spread(t, target, by_left, block):
+            row = pl.multiple_of(lax.rem(t, own) * beams, beams)
+            for p in range(polars):
+                for half in range(halves):
+                    for q in range(polars):
+                        where = pl.ds(
+                            (p * halves + half) * polars + q, beams,
+                            stride=polars * polars * halves,
+                        )
+                        value = scales[block, p if by_left else q, pl.ds(row, beams), :]
+                        target[t, where, :] = value * (1.0 / frames) if by_left else value
+
+        def left_step(t, carry):
+            spread(t, lrows, True, me)
+            return carry
+
+        def right_step(t, carry):
+            spread(t, rrows, False, t // own)
+            return carry
+
+        lax.fori_loop(0, own, left_step, 0)
+        lax.fori_loop(0, n * own, right_step, 0)
+        for copy in row_copies():
+            copy.start()
 
     def widen(block, c, target):
         def step(i, carry):
@@ -310,7 +376,7 @@
 
     def out_copy(slot, c, s, block):
         return pltpu.make_async_copy(
-            stage.at[slot], out.at[:, c, s, pl.ds(block * own, own)], o_sem.at[slot]
+            stage.at[slot], out.at[:, c, s, pl.ds(block * (own // 2), own // 2)], o_sem.at[slot]
         )
 
     def correlate(c, block, first):
@@ -326,43 +392,60 @@
             else:
                 out_copy(slot, c, s, block).wait()
 
-            def pair(t, inner_carry):
-                trow = pl.multiple_of(t * beams, beams)
-                for half in range(halves):
-                    lanes = pl.ds(half * LANES, LANES)
-                    re = {}
-                    im = {}
-                    for f in range(frames):
+            def pair(i, inner_carry):
+                half = i % halves
+                t = i // halves
+                lanes = pl.ds(pl.multiple_of(half * LANES, LANES), LANES)
+                trows = [pl.multiple_of((2 * t + x) * beams, beams) for x in range(2)]
+
+                def some_frames(k, totals):
+                    totals = list(totals)
+                    for j in range(unroll):
+                        f = k * unroll + j
                         lre = [left[p, f, pl.ds(srow, beams), lanes] for p in range(polars)]
                         lim = [
                             left[p, f, pl.ds(half_rows + srow, beams), lanes]
                             for p in range(polars)
                         ]
-                        rre = [right[q, f, pl.ds(trow, beams), lanes] for q in range(polars)]
-                        rim = [
-                            right[q, f, pl.ds(half_rows + trow, beams), lanes]
-                            for q in range(polars)
-                        ]
-                        for p in range(polars):
-                            for q in range(polars):
-                                a = lre[p] * rre[q] + lim[p] * rim[q]
-                                b = lim[p] * rre[q] - lre[p] * rim[q]
-                                re[p, q] = a if f == 0 else re[p, q] + a
-                                im[p, q] = b if f == 0 else im[p, q] + b
+                        for x in range(2):
+                            rre = [
+                                right[q, f, pl.ds(trows[x], beams), lanes] for q in range(polars)
+                            ]
+                            rim = [
+                                right[q, f, pl.ds(half_rows + trows[x], beams), lanes]
+                                for q in range(polars)
+                            ]
+                            for p in range(polars):
+                                for q in range(polars):
+                                    at = ((x * polars + p) * polars + q) * 2
+                                    totals[at] += lre[p] * rre[q] + lim[p] * rim[q]
+                                    totals[at + 1] += lim[p] * rre[q] - lre[p] * rim[q]
+                    return tuple(totals)
+
+                zero = jnp.zeros((beams, LANES), jnp.float32)
+                totals = lax.fori_loop(
+                    0, frames // unroll, some_frames, (zero,) * (4 * polars * polars)
+                )
+                for x in range(2):
                     for p in range(polars):
-                        for q in range(polars):
-                            scale = (
-                                scales[me, p, pl.ds(srow, beams), :]
-                                * scales[block, q, pl.ds(trow, beams), :]
-                                * (1.0 / frames)
+                        low = pl.multiple_of(
+                            (p * halves + half) * (polars * beams), polars * beams
+                        )
+                        for o in range(2):
+                            value = jnp.concatenate(
+                                [
+                                    totals[((x * polars + p) * polars + q) * 2 + o]
+                                    for q in range(polars)
+                                ],
+                                axis=0,
                             )
-                            row = (p * halves + half) * polars + q
-                            where = pl.ds(row, beams, stride=polars * polars * halves)
-                            stage[slot, 0, t, where, :] = re[p, q] * scale
-                            stage[slot, 1, t, where, :] = im[p, q] * scale
+                            stage[
+                                slot, o, t, pl.ds(low, polars * beams),
+                                x * LANES : (x + 1) * LANES,
+                            ] = value.astype(jnp.bfloat16)
                 return inner_carry
 
-            lax.fori_loop(0, own, pair, 0)
+            lax.fori_loop(0, (own // 2) * halves, pair, 0)
             out_copy(slot, c, s, block).start()
             return carry
 
@@ -372,46 +455,88 @@
         if step == 0:
             return me
         two_sided = jnp.minimum(me, n - 1 - me)
+        way = jnp.where(low_side, 1, -1)
         near = (step + 1) // 2
-        near_block = me - near if step % 2 else me + near
-        far = step - two_sided
-        far_block = jnp.where(me < n - 1 - me, me + far, me - far)
+        near_block = me - way * near if step % 2 else me + way * near
+        far_block = me + way * (step - two_sided)
         return jnp.where(step <= 2 * two_sided, near_block, far_block)
 
-    for chunk in range(polars):
-        chunk_work(chunk)
+    def unit(c, step):
+        if step == 0:
+            widen(me, c, left)
+        else:
+            for p in range(polars):
+                arrive(step, c * polars + p)
+        correlate(c, order(step), c == 0 and step == 0)
+
+    last = coarse - 1
+    hops = range(1, n - 1)
+    ps = range(polars)
+
+    def take_near(c, p):
+        for distance in hops:
+            receive(outward, distance, c * polars + p)
+
+    def give_near(c, p):
+        for distance in hops:
+            launch(outward, distance, c * polars + p)
+
+    def pass_far(c, p, distances):
+        for distance in distances:
+            receive(inward_end, distance, c * polars + p)
+            launch(inward_end, distance, c * polars + p)
+
+    for p in ps:
+        chunk_work(p)
+    unit(0, 0)
     for c in range(1, coarse):
-        for p in range(polars):
+        prev = c - 1
+        for p in ps:
             chunk_work(c * polars + p)
-            for q in range(polars):
-                if p == 0:
-                    pass_on(1, (c - 1) * polars + q)
-        for distance in range(2, n - 1):
-            for q in range(polars):
-                pass_on(distance, (c - 1) * polars + q)
-    power_work()
-    widen(me, 0, left)
-    last = coarse - 1
-    for c in range(coarse):
-        if c:
-            widen(me, c, left)
-        for step in range(n):
-            if step >= 1:
-                for q in range(polars):
-                    arrive(step, c * polars + q)
-            if c == last and coarse == 1 and step == 0:
-                for distance in range(1, n - 1):
-                    for q in range(polars):
-                        pass_on(distance, c * polars + q)
-            correlate(c, order(step), c == 0 and step == 0)
-            if c == last - 1 and step >= n - 2:
-                for q in range(polars):
-                    if step == n - 2:
-                        pass_on(1, last * polars + q)
-            if c == last - 1 and step == n - 1:
-                for distance in range(2, n - 1):
-                    for q in range(polars):
-                        pass_on(distance, last * polars + q)
+            launch(outward, 0, prev * polars + p)
+        if c == last:
+            power_start()
+        for p in ps:
+            take_near(prev, p)
+        unit(prev, 1)
+        for p in ps:
+            give_near(prev, p)
+            pass_far(prev, p, hops[:1])
+        if c == last:
+            power_finish()
+        if n > 2:
+            unit(prev, 2)
+        for p in ps:
+            if c == last:
+                launch(outward, 0, last * polars + p)
+            pass_far(prev, p, hops[1:])
+        for step in range(3, n):
+            unit(prev, step)
+        if c < last:
+            unit(c, 0)
+    if coarse == 1:
+        power_start()
+        for p in ps:
+            launch(outward, 0, p)
+        power_finish()
+    for p in ps:
+        take_near(last, p)
+        give_near(last, p)
+        pass_far(last, p, hops[:1])
+    if coarse > 1:
+        unit(last, 0)
+    for p in ps:
+        pass_far(last, p, hops[1:])
+        if p == 0 and n > 2:
+            unit(last, 1)
+    for step in range(1 if n == 2 else 2, n):
+        if step == n - 1:
+            scale_rows()
+        unit(last, step)
+    drain(outward)
+    drain(inward_end)
+    for copy in row_copies():
+        copy.wait()
 
     for slot in range(2):
         out_copy(slot, last, own - 2 + slot, order(n - 1)).wait()
@@ -428,15 +553,14 @@
         for chunk in range(chunks):
             halo(chunk).wait_send()
 
-    for distance in range(n - 1):
-        for chunk in range(chunks):
-            @pl.when(jnp.logical_and(me - distance >= 0, me < n - 1))
-            def _():
-                beam_copy(me - distance, chunk, True, distance).wait_send()
-
-            @pl.when(jnp.logical_and(me + distance < n, me > 0))
-            def _():
-                beam_copy(me + distance, chunk, False, distance).wait_send()
+    for chunk in range(chunks):
+        @pl.when(me == 0)
+        def _():
+            beam_copy(me, chunk, True, 0).wait_send()
+
+        @pl.when(me == n - 1)
+        def _():
+            beam_copy(me, chunk, False, 0).wait_send()
 
 
 def chain(volts, perm, steer, fir_taps, table, beams):
@@ -456,8 +580,12 @@
     return pl.pallas_call(
         functools.partial(chain_kernel, beams),
         in_specs=[pl.BlockSpec(memory_space=pl.ANY), vmem, vmem, vmem, vmem],
-        out_specs=pl.BlockSpec(memory_space=pl.ANY),
-        out_shape=jax.ShapeDtypeStruct((2, coarse, own, n * own, out_rows, LANES), f32),
+        out_specs=[pl.BlockSpec(memory_space=pl.ANY)] * 3,
+        out_shape=[
+            jax.ShapeDtypeStruct((2, coarse, own, n * own // 2, out_rows, 2 * LANES), bf16),
+            jax.ShapeDtypeStruct((own, out_rows, LANES), f32),
+            jax.ShapeDtypeStruct((n * own, out_rows, LANES), f32),
+        ],
         scratch_shapes=[
             pltpu.VMEM((2, frames, 2, dishes, fine), bf16),
             pltpu.VMEM((chunks, n, frames, 2, share, fine), bf16),
@@ -470,9 +598,11 @@
             pltpu.VMEM((polars, half_rows, fine), f32),
             pltpu.VMEM((n_chan, polars, half_rows, LANES), f32),
             pltpu.VMEM((n, polars, half_rows, LANES), f32),
+            pltpu.VMEM((own, out_rows, LANES), f32),
+            pltpu.VMEM((n * own, out_rows, LANES), f32),
             pltpu.VMEM((polars, frames, rows, fine), f32),
             pltpu.VMEM((polars, frames, rows, fine), f32),
-            pltpu.VMEM((2, 2, own, out_rows, LANES), f32),
+            pltpu.VMEM((2, 2, own // 2, out_rows, 2 * LANES), bf16),
             dma((2,)),
             dma((chunks, n - 1)),
             dma((chunks, n - 1)),
@@ -487,6 +617,7 @@
             dma((n - 1,)),
             dma((n - 1,)),
             dma((2,)),
+            dma((2,)),
         ],
         compiler_params=pltpu.CompilerParams(
             vmem_limit_bytes=VMEM_LIMIT, collective_id=0, has_side_effects=True
@@ -496,6 +627,50 @@
         ),
         name="chain",
     )(volts, perm, steer, fir_taps, table)
+
+
+def scaling_kernel(x_ref, order_ref, left_ref, right_ref, out_ref):
+    _, _, stations, pairs, rows, lanes = x_ref.shape
+    group = order_ref.shape[0] // rows
+
+    def station(s, carry):
+        left = left_ref[s]
+        for i in range(pairs // group):
+            block = x_ref[0, 0, s, i * group : (i + 1) * group].reshape(group * rows, lanes)
+            values = jnp.dot(order_ref[...], block, preferred_element_type=jnp.float32)
+            for g in range(group):
+                for x in range(2):
+                    t = (i * group + g) * 2 + x
+                    value = values[g * rows : (g + 1) * rows, x * LANES : (x + 1) * LANES]
+                    out_ref[0, 0, s, t] = value * (left * right_ref[t])
+        return carry
+
+    lax.fori_loop(0, stations, station, 0)
+
+
+def scaled(values, order, lrows, rrows):
+    parts, coarse, own, pairs, rows, lanes = values.shape
+    shape = (parts, coarse, own, 2 * pairs, rows, LANES)
+    some = own // 2
+    return pl.pallas_call(
+        scaling_kernel,
+        grid=(parts, coarse, own // some),
+        in_specs=[
+            pl.BlockSpec((1, 1, some, pairs, rows, lanes), lambda o, c, s: (o, c, s, 0, 0, 0)),
+            pl.BlockSpec(order.shape, lambda o, c, s: (0, 0)),
+            pl.BlockSpec((some, rows, LANES), lambda o, c, s: (s, 0, 0)),
+            pl.BlockSpec(rrows.shape, lambda o, c, s: (0, 0, 0)),
+        ],
+        out_specs=pl.BlockSpec(
+            (1, 1, some, 2 * pairs, rows, LANES), lambda o, c, s: (o, c, s, 0, 0, 0)
+        ),
+        out_shape=jax.ShapeDtypeStruct(shape, jnp.float32),
+        compiler_params=pltpu.CompilerParams(vmem_limit_bytes=VMEM_LIMIT),
+        cost_estimate=pl.CostEstimate(
+            flops=values.size * 2 * rows, bytes_accessed=values.size * 6, transcendentals=0
+        ),
+        name="scaled",
+    )(values, order, lrows, rrows)
 
 
 def per_device(voltages, fir_taps, station_map, beam_index, weight_table):
@@ -530,8 +705,14 @@
     steer = jnp.transpose(steer, (3, 2, 0, 4, 1, 5, 6))
     steer = steer.reshape(n, coarse_dev, 2 * share, 2 * own * beams)
     volts = jnp.transpose(voltages, (1, 4, 3, 0, 2, 5))
-    result = chain(volts, perm, steer, fir_taps, dft_table(fine), beams)
     halves = fine // LANES
+    count = beams * polars * polars * halves
+    final = np.arange(count)
+    source = final % (count // beams) * beams + final // (count // beams)
+    ordering = np.kron(np.eye(2), source[:, None] == final[None, :])
+    ordering = jnp.asarray(ordering, jnp.bfloat16)
+    result, lrows, rrows = chain(volts, perm, steer, fir_taps, dft_table(fine), beams)
+    result = scaled(result, ordering, lrows, rrows)
     result = result.reshape(
         2, coarse_dev, own, total_stations, beams, polars, halves, polars, LANES
     )

time: 532 us -> 476 us (0.89)
  Pallas kernels: 489 us -> 459 us
  local copies, waits for them, and re-layouts: 36.4 us -> 13.8 us
    pallas_call x1, Pallas kernels: 489 us -> 438 us  [chain(): pl.pallas_call(functools.partial(chain_kernel, beams), in_specs=[pl.Block...]
    unnamed x6 -> x5, local copies, waits for them, and re-layouts: 34.9 us -> 12.3 us
    pallas_call x0 -> x1, Pallas kernels: none -> 20.5 us  [scaled(): pl.pallas_call(scaling_kernel, grid=(parts, coarse, own // some), in_spec...]
where the time goes in v2:
time: 476 us
  Pallas kernels  459 us (96%)
  local copies, waits for them, and re-layouts  13.8 us (3%)
    pallas_call x1, Pallas kernels, chain(): pl.pallas_call(functools.partial(chain_kernel, beams), in_specs=[pl.Block...  438 us
    pallas_call x1, Pallas kernels, scaled(): pl.pallas_call(scaling_kernel, grid=(parts, coarse, own // some), in_spec...  20.5 us
    unnamed x5, local copies, waits for them, and re-layouts  12.3 us

profile of v2, /device:TPU:0, one launch (start us, length us, event | category | flops | bytes accessed | tf_op | source)
XLA Modules:
  0.0 475.6 jit_solution(8589947182808649192)
XLA Ops:
  0.0 0.0 copy-start
  0.0 0.7 copy-done
  0.7 0.7 multiply_subtract_fusion
  1.4 0.2 convert_reduce_fusion
  1.5 0.8 select_reduce_fusion.1
  2.3 0.1 eq.61
  2.4 0.1 fusion.2
  2.6 0.1 stack.16
  2.7 0.1 stack.14
  2.7 0.1 maximum_bitcast_fusion
  2.8 0.1 copy.18
  2.9 0.6 fusion.perm
  3.5 0.1 broadcast_in_dim.62
  3.6 0.2 broadcast_in_dim.63
  3.9 0.1 copy.17
  4.0 0.3 broadcast_in_dim.68
  4.3 0.3 broadcast_in_dim.69
  4.6 0.1 copy.19
  4.7 0.7 broadcast_select_fusion.steer
  5.4 11.6 %copy.22 = bf16[2,2,128,16,2,256]{5,2,0,3,4,1:T(8,128)(2,1)} copy(bf16[2,2,128,16,2,256]{5,4,3,2,1,0:T(2,128)(2,1)} %param.7) | data formatting | bytes 16777216 | tf_op args[0]
  16.9 438.1 %chain.1 = (bf16[2,2,8,16,64,256]{5,4,3,2,1,0:T(8,128)(2,1)}, f32[8,64,128]{2,1,0:T(8,128)}, f32[32,64,128]{2,1,0:T(8,128)}) custom-call(bf16[2,2,16,2,128,256]{5,4,3,2,1,0:T(8,128)(2,1)} %bitcast.32, bf16[128,128]{1,0:T(8,128)(2,1)} %fusion.perm, bf16[4,2,64,128]{3,2,1,0:T(8,128)(2,1)} %broadcast_select_fusion.steer, f32[16,256]{1,0:T(8,128)} %taps.1, ...), custom_call_target="tpu_custom_call" | custom-call | flops 53687091200 | bytes 33554432 | tf_op jit(solution)/shard_map/chain/pallas_call | solution.py:580
  455.0 0.0 copy-start.1
  455.1 20.5 %scaled.1 = f32[2,2,8,32,64,128]{5,4,3,2,1,0:T(8,128)} custom-call(bf16[2,2,8,16,64,256]{5,4,3,2,1,0:T(8,128)(2,1)} %get-tuple-element.8.x_ref, bf16[128,128]{1,0:T(8,128)(2,1)} %constant.27.clone.order_ref, f32[8,64,128]{2,1,0:T(8,128)} %get-tuple-element.9.left_ref, f32[32,64,128]{2,1,0:T(8,128)} %get-tuple-element.10.right_ref), custom_call_target="tpu_custom_call" | custom-call | flops 1073741824 | bytes 50331648 | tf_op jit(solution)/shard_map/scaled/pallas_call | solution.py:655
  475.6 0.0 copy-done.1
  (5 shorter events, 0.0 us)
Async XLA Ops:
  0.0 0.7 copy-start
  455.0 20.5 %copy-start.1 = (bf16[2,16,2,8]{1,3,2,0:T(8,128)(2,1)S(1)}, bf16[2,16,2,8]{1,3,2,0:T(8,128)(2,1)}, u32[]{:S(2)}) copy-start(bf16[2,16,2,8]{1,3,2,0:T(8,128)(2,1)} %param.11) | copy-start | bytes 3076

commit v3 on v2

--- a/solution.py
+++ b/solution.py
@@ -28,8 +28,9 @@
 def chain_kernel(
     beams, volts, perm, steer, taps, dft, out, lout, rout,
     xin, send, recv, srecv, sfull, ybuf, fil, gbuf, pacc, pwx, scales, lrows, rrows, left, right, stage,
+    relay, srelay, srelay_full, part,
     load_sem, a_send, a_recv, s_send, s_recv, h_send, h_recv,
-    b_send, b_recv, p_send, p_recv, c_send, c_recv, o_sem, r_sem,
+    b_send, b_recv, p_send, p_recv, c_send, c_recv, o_sem, r_sem, q_send, q_recv, t_send, t_recv, v_send, v_recv,
 ):
     coarse, polars, frames, _, dishes, fine = volts.shape
     chunks = coarse * polars
@@ -49,6 +50,8 @@
     group = 4
     unroll = 8
     ahead = 2
+    base = polars if coarse > 1 and n > 3 else chunks
+    ends = ((True, 0, 1), (False, n - 1, n - 2))
 
     barrier = pltpu.get_barrier_semaphore()
     for k in range(1, n):
@@ -101,15 +104,63 @@
             device_id={"stn": lax.rem(me + k, n)}, device_id_type=MESH,
         )
 
+    def relay_copy(chunk, low, end, target):
+        slot = me - 1 if low else me
+        return pltpu.make_async_remote_copy(
+            src_ref=send.at[chunk, end], dst_ref=relay.at[chunk - base, slot],
+            send_sem=q_send.at[chunk - base, int(low)], recv_sem=q_recv.at[chunk - base, slot],
+            device_id={"stn": jnp.int32(target)}, device_id_type=MESH,
+        )
+
+    def relay_arrival(chunk, slot):
+        return pltpu.make_async_remote_copy(
+            src_ref=send.at[chunk, me], dst_ref=relay.at[chunk - base, slot],
+            send_sem=q_send.at[chunk - base, 0], recv_sem=q_recv.at[chunk - base, slot],
+            device_id={"stn": lax.rem(me + 1, n)}, device_id_type=MESH,
+        )
+
+    def steer_relay(low, end, target):
+        slot = me - 1 if low else me
+        return pltpu.make_async_remote_copy(
+            src_ref=steer.at[end], dst_ref=srelay.at[slot],
+            send_sem=t_send.at[int(low)], recv_sem=t_recv.at[slot],
+            device_id={"stn": jnp.int32(target)}, device_id_type=MESH,
+        )
+
+    def steer_relay_arrival(slot):
+        return pltpu.make_async_remote_copy(
+            src_ref=steer.at[me], dst_ref=srelay.at[slot],
+            send_sem=t_send.at[0], recv_sem=t_recv.at[slot],
+            device_id={"stn": lax.rem(me + 1, n)}, device_id_type=MESH,
+        )
+
+    def part_copy(chunk, end):
+        return pltpu.make_async_remote_copy(
+            src_ref=part.at[chunk - base], dst_ref=part.at[chunk - base],
+            send_sem=v_send.at[chunk - base], recv_sem=v_recv.at[chunk - base],
+            device_id={"stn": jnp.int32(end)}, device_id_type=MESH,
+        )
+
+    def past_neighbour(low):
+        return me >= 2 if low else me <= n - 3
+
+    at_end = jnp.logical_or(me == 0, me == n - 1)
+
     def send_dishes(chunk):
         for distance in range(1, n):
-            @pl.when(me + distance < n)
+            @pl.when(me + distance < (n if chunk < base else n - 1))
             def _():
                 dish_copy(chunk, distance).start()
 
-            @pl.when(me - distance >= 0)
+            @pl.when(me - distance >= (0 if chunk < base else 1))
             def _():
                 dish_copy(chunk, n - distance).start()
+
+        if chunk >= base:
+            for low, end, target in ends:
+                @pl.when(past_neighbour(low))
+                def _():
+                    relay_copy(chunk, low, end, target).start()
 
     load(0).start()
     srecv[me] = steer[me]
@@ -134,6 +185,11 @@
             pl.semaphore_wait(barrier, (n - 1) + (n_chan - 1) + (n_tm - 1))
             for k in range(1, n):
                 steer_copy(k).start()
+            if base < chunks:
+                for low, end, target in ends:
+                    @pl.when(past_neighbour(low))
+                    def _():
+                        steer_relay(low, end, target).start()
         if chunk < ahead:
             send_dishes(chunk)
 
@@ -160,6 +216,58 @@
     for c in range(coarse):
         columns = srecv[:, c].astype(jnp.float32).reshape(n * 2 * share, rows)
         sfull[c] = jnp.transpose(columns).astype(jnp.bfloat16)
+
+    def prepare_relay(low, end, target):
+        mine = 0 if low else n - 2
+        srelay[mine] = steer[end]
+        for slot in range(n - 1):
+            if slot != mine:
+                steer_relay_arrival(slot).wait_recv()
+        for c in range(1, coarse):
+            columns = srelay[:, c].astype(jnp.float32).reshape((n - 1) * 2 * share, rows)
+            srelay_full[c - 1] = jnp.transpose(columns).astype(jnp.bfloat16)
+
+        def own_step(i, carry):
+            for chunk in range(base, chunks):
+                relay[chunk - base, mine, i] = send[chunk, end, i]
+            return carry
+
+        lax.fori_loop(0, frames, own_step, 0)
+
+    def relay_work(chunk, low, end):
+        mine = 0 if low else n - 2
+        for slot in range(n - 1):
+            if slot != mine:
+                relay_arrival(chunk, slot).wait_recv()
+
+        def relay_step(frame, carry):
+            terms = relay[chunk - base, :, frame].reshape(-1, fine)
+            total = jnp.dot(
+                srelay_full[chunk // polars - 1], terms, preferred_element_type=jnp.float32
+            )
+            part[chunk - base, frame] = total.astype(jnp.bfloat16)
+            return carry
+
+        lax.fori_loop(0, frames, relay_step, 0)
+        part_copy(chunk, end).start()
+
+    if base < chunks:
+        for low, end, target in ends:
+            @pl.when(me == target)
+            def _():
+                prepare_relay(low, end, target)
+
+        @pl.when(at_end)
+        def _():
+            def blank_step(i, carry):
+                for chunk in range(base, chunks):
+                    for k in range(1, n):
+                        recv[chunk, lax.rem(me + k, n), i] = jnp.zeros(
+                            (2, share, fine), jnp.bfloat16
+                        )
+                return carry
+
+            lax.fori_loop(0, frames, blank_step, 0)
 
     def halo(chunk):
         return pltpu.make_async_remote_copy(
@@ -212,8 +320,16 @@
 
     def chunk_work(chunk):
         c, p = chunk // polars, chunk % polars
-        for k in range(1, n):
-            dish_arrival(chunk, k).wait_recv()
+        relayed = chunk >= base
+
+        def arrivals():
+            for k in range(1, n):
+                dish_arrival(chunk, k).wait_recv()
+
+        if relayed:
+            pl.when(jnp.logical_not(at_end))(arrivals)
+        else:
+            arrivals()
         if chunk + ahead < chunks:
             send_dishes(chunk + ahead)
 
@@ -227,7 +343,25 @@
             ybuf[chunk, history + frame] = formed.astype(jnp.bfloat16)
             return carry
 
-        lax.fori_loop(0, frames, beam_step, 0)
+        def end_step(frame, carry):
+            terms = recv[chunk, :, frame].reshape(-1, fine)
+            formed = jnp.dot(sfull[c], terms, preferred_element_type=jnp.float32)
+            formed = formed + part[chunk - base, frame].astype(jnp.float32)
+            ybuf[chunk, history + frame] = formed.astype(jnp.bfloat16)
+            return carry
+
+        if relayed:
+            @pl.when(at_end)
+            def _():
+                part_copy(chunk, 0).wait_recv()
+                lax.fori_loop(0, frames, end_step, 0)
+
+            @pl.when(jnp.logical_not(at_end))
+            def _():
+                lax.fori_loop(0, frames, beam_step, 0)
+
+        else:
+            lax.fori_loop(0, frames, beam_step, 0)
 
         @pl.when(tm < n_tm - 1)
         def _():
@@ -237,20 +371,20 @@
         def _():
             halo(chunk).wait_recv()
 
-        part = min(32, half_rows)
+        band = min(32, half_rows)
 
         def filter_step(i, carry):
             for j in range(group):
                 frame = i * group + j
                 for o in range(2):
-                    for low in range(0, half_rows, part):
+                    for low in range(0, half_rows, band):
                         start = o * half_rows + low
-                        total = jnp.zeros((part, fine), jnp.float32)
+                        total = jnp.zeros((band, fine), jnp.float32)
                         for tap in range(n_taps):
-                            sample = ybuf[chunk, frame + (history - tap), start : start + part, :]
+                            sample = ybuf[chunk, frame + (history - tap), start : start + band, :]
                             total = total + taps[tap : tap + 1, :] * sample.astype(jnp.float32)
                         fil[
-                            j * half_rows + low : j * half_rows + low + part,
+                            j * half_rows + low : j * half_rows + low + band,
                             o * fine : (o + 1) * fine,
                         ] = total.astype(jnp.bfloat16)
             spec = jnp.dot(fil[...], dft[...], preferred_element_type=jnp.float32)
@@ -274,6 +408,11 @@
             beam_copy(me, chunk, False, 0).start()
 
         launch(inward_end, 0, chunk)
+        if relayed:
+            for low, end, target in ends:
+                @pl.when(me == target)
+                def _():
+                    relay_work(chunk, low, end)
 
     def arrive(distance, chunk):
         @pl.when(me == n - 1)
@@ -461,10 +600,13 @@
         far_block = me + way * (step - two_sided)
         return jnp.where(step <= 2 * two_sided, near_block, far_block)
 
+    wide_of = []
+
     def unit(c, step):
-        if step == 0:
+        if wide_of[-1:] != [c]:
             widen(me, c, left)
-        else:
+            wide_of.append(c)
+        if step:
             for p in range(polars):
                 arrive(step, c * polars + p)
         correlate(c, order(step), c == 0 and step == 0)
@@ -500,39 +642,53 @@
             take_near(prev, p)
         unit(prev, 1)
         for p in ps:
-            give_near(prev, p)
+            if c == last:
+                launch(outward, 0, last * polars + p)
             pass_far(prev, p, hops[:1])
         if c == last:
             power_finish()
         if n > 2:
             unit(prev, 2)
+        if c < last:
+            for p in ps:
+                give_near(prev, p)
+                pass_far(prev, p, hops[1:])
+            for step in range(3, n):
+                unit(prev, step)
+            unit(c, 0)
+    prev = last - 1
+    if coarse == 1:
+        power_start()
+        power_finish()
         for p in ps:
-            if c == last:
-                launch(outward, 0, last * polars + p)
+            launch(outward, 0, p)
+            take_near(last, p)
+            give_near(last, p)
+            pass_far(last, p, hops)
+        for step in range(1, n - 1):
+            unit(last, step)
+    else:
+        for p in ps:
+            give_near(prev, p)
+            pass_far(last, p, hops[:1])
+            if p < n - 1:
+                unit(last, p)
+            if p == 0:
+                for q in ps:
+                    take_near(last, q)
+        for p in ps:
+            give_near(last, p)
             pass_far(prev, p, hops[1:])
+            if p == 0:
+                for step in range(polars, n - 1):
+                    unit(last, step)
+        pass_far(last, 0, hops[1:])
         for step in range(3, n):
             unit(prev, step)
-        if c < last:
-            unit(c, 0)
-    if coarse == 1:
-        power_start()
-        for p in ps:
-            launch(outward, 0, p)
-        power_finish()
-    for p in ps:
-        take_near(last, p)
-        give_near(last, p)
-        pass_far(last, p, hops[:1])
-    if coarse > 1:
-        unit(last, 0)
-    for p in ps:
-        pass_far(last, p, hops[1:])
-        if p == 0 and n > 2:
-            unit(last, 1)
-    for step in range(1 if n == 2 else 2, n):
-        if step == n - 1:
-            scale_rows()
-        unit(last, step)
+        for p in ps[1:]:
+            pass_far(last, p, hops[1:])
+    scale_rows()
+    unit(last, n - 1)
     drain(outward)
     drain(inward_end)
     for copy in row_copies():
@@ -543,10 +699,27 @@
     for k in range(1, n):
         steer_copy(k).wait_send()
         scale_copy(k).wait_send()
-        for chunk in range(chunks):
+        to_end = jnp.logical_or(lax.rem(me + k, n) == 0, lax.rem(me + k, n) == n - 1)
+        for chunk in range(base):
             dish_copy(chunk, k).wait_send()
+        for chunk in range(base, chunks):
+            @pl.when(jnp.logical_not(to_end))
+            def _():
+                dish_copy(chunk, k).wait_send()
     for k in range(1, n_chan):
         power_copy(k).wait_send()
+    if base < chunks:
+        for low, end, target in ends:
+            @pl.when(past_neighbour(low))
+            def _():
+                steer_relay(low, end, target).wait_send()
+                for chunk in range(base, chunks):
+                    relay_copy(chunk, low, end, target).wait_send()
+
+            @pl.when(me == target)
+            def _():
+                for chunk in range(base, chunks):
+                    part_copy(chunk, end).wait_send()
 
     @pl.when(tm < n_tm - 1)
     def _():
@@ -574,6 +747,9 @@
     out_rows = beams * polars * polars * (fine // LANES)
     history = fir_taps.shape[0] - 1
     dma = pltpu.SemaphoreType.DMA
+    late = chunks - polars if coarse > 1 and n > 3 else 1
+    late_shape = (frames, 2, share, fine) if coarse > 1 and n > 3 else (1, 1, 16, fine)
+    late_c = max(coarse - 1, 1)
     bf16, f32 = jnp.bfloat16, jnp.float32
     size = 2 * coarse * own * n * own * out_rows * LANES
     vmem = pl.BlockSpec(memory_space=pltpu.VMEM)
@@ -603,6 +779,10 @@
             pltpu.VMEM((polars, frames, rows, fine), f32),
             pltpu.VMEM((polars, frames, rows, fine), f32),
             pltpu.VMEM((2, 2, own // 2, out_rows, 2 * LANES), bf16),
+            pltpu.VMEM((late, n - 1) + late_shape, bf16),
+            pltpu.VMEM((n - 1, coarse, terms, rows), bf16),
+            pltpu.VMEM((late_c, rows, (n - 1) * terms), bf16),
+            pltpu.VMEM((late, late_shape[0], rows, fine), bf16),
             dma((2,)),
             dma((chunks, n - 1)),
             dma((chunks, n - 1)),
@@ -618,6 +798,12 @@
             dma((n - 1,)),
             dma((2,)),
             dma((2,)),
+            dma((late, 2)),
+            dma((late, n - 1)),
+            dma((2,)),
+            dma((n - 1,)),
+            dma((late,)),
+            dma((late,)),
         ],
         compiler_params=pltpu.CompilerParams(
             vmem_limit_bytes=VMEM_LIMIT, collective_id=0, has_side_effects=True

time: 476 us -> 477 us (level)
  no operation moved by 1% of the time
where the time goes in v3:
time: 477 us
  Pallas kernels  460 us (96%)
  local copies, waits for them, and re-layouts  13.8 us (3%)
    pallas_call x1, Pallas kernels, chain(): pl.pallas_call(functools.partial(chain_kernel, beams), in_specs=[pl.Block...  440 us
    pallas_call x1, Pallas kernels, scaled(): pl.pallas_call(scaling_kernel, grid=(parts, coarse, own // some), in_spec...  20.5 us
    unnamed x5, local copies, waits for them, and re-layouts  12.3 us

profile of v3, /device:TPU:0, one launch (start us, length us, event | category | flops | bytes accessed | tf_op | source)
XLA Modules:
  0.0 477.0 jit_solution(614690118789141961)
XLA Ops:
  0.0 0.0 copy-start
  0.0 0.7 copy-done
  0.7 0.7 multiply_subtract_fusion
  1.4 0.2 convert_reduce_fusion
  1.5 0.8 select_reduce_fusion.1
  2.3 0.1 eq.61
  2.4 0.1 fusion.2
  2.6 0.1 stack.16
  2.7 0.1 stack.14
  2.7 0.1 maximum_bitcast_fusion
  2.8 0.1 copy.18
  2.9 0.6 fusion.perm
  3.5 0.1 broadcast_in_dim.62
  3.6 0.2 broadcast_in_dim.63
  3.9 0.1 copy.17
  4.0 0.3 broadcast_in_dim.68
  4.3 0.3 broadcast_in_dim.69
  4.6 0.1 copy.19
  4.7 0.7 broadcast_select_fusion.steer
  5.4 11.6 %copy.22 = bf16[2,2,128,16,2,256]{5,2,0,3,4,1:T(8,128)(2,1)} copy(bf16[2,2,128,16,2,256]{5,4,3,2,1,0:T(2,128)(2,1)} %param.7) | data formatting | bytes 16777216 | tf_op args[0]
  16.9 439.6 %chain.1 = (bf16[2,2,8,16,64,256]{5,4,3,2,1,0:T(8,128)(2,1)}, f32[8,64,128]{2,1,0:T(8,128)}, f32[32,64,128]{2,1,0:T(8,128)}) custom-call(bf16[2,2,16,2,128,256]{5,4,3,2,1,0:T(8,128)(2,1)} %bitcast.32, bf16[128,128]{1,0:T(8,128)(2,1)} %fusion.perm, bf16[4,2,64,128]{3,2,1,0:T(8,128)(2,1)} %broadcast_select_fusion.steer, f32[16,256]{1,0:T(8,128)} %taps.1, ...), custom_call_target="tpu_custom_call" | custom-call | flops 53687091200 | bytes 33554432 | tf_op jit(solution)/shard_map/chain/pallas_call | solution.py:756
  456.5 0.0 copy-start.1
  456.5 20.5 %scaled.1 = f32[2,2,8,32,64,128]{5,4,3,2,1,0:T(8,128)} custom-call(bf16[2,2,8,16,64,256]{5,4,3,2,1,0:T(8,128)(2,1)} %get-tuple-element.8.x_ref, bf16[128,128]{1,0:T(8,128)(2,1)} %constant.27.clone.order_ref, f32[8,64,128]{2,1,0:T(8,128)} %get-tuple-element.9.left_ref, f32[32,64,128]{2,1,0:T(8,128)} %get-tuple-element.10.right_ref), custom_call_target="tpu_custom_call" | custom-call | flops 1073741824 | bytes 50331648 | tf_op jit(solution)/shard_map/scaled/pallas_call | solution.py:841
  477.0 0.0 copy-done.1
  (5 shorter events, 0.0 us)
Async XLA Ops:
  0.0 0.7 copy-start
  456.5 20.5 %copy-start.1 = (bf16[2,16,2,8]{1,3,2,0:T(8,128)(2,1)S(1)}, bf16[2,16,2,8]{1,3,2,0:T(8,128)(2,1)}, u32[]{:S(2)}) copy-start(bf16[2,16,2,8]{1,3,2,0:T(8,128)(2,1)} %param.11) | copy-start | bytes 3076
